TPU v7x, 256 devices: a whole 4x4x8 slice. The times are simulated.
256 devices in a mesh: gx: 16 (over y_hi, z), gy: 16 (over y_lo, x, core).
Axes of the slice: x: 4, y: 4 (y_hi: 2, y_lo: 2; y = y_hi * 2 + y_lo), z: 8, core: 2. Of those that a mesh axis runs over, the one named last changes fastest.
Arguments:
- hidden: bfloat16 [8192, 14336], P('gx', 'gy'), may hold values from -6 to 6
- weight: bfloat16 [4096, 14336], P(None, 'gy'), may hold values from -0.0625 to 0.0625
- cotangent: bfloat16 [8192, 4096], P('gx', 'gy'), may hold values from -6 to 6
Outputs:
- output: bfloat16 [8192, 4096], P('gx', 'gy')
- hidden_grad: bfloat16 [8192, 14336], P('gx', 'gy')
- weight_grad: float32 [4096, 14336], P('gx', 'gy')
All inputs are finite; a program needn't handle non-finite values.
Results may differ from a plain program's by a relative error of at most 0.001.
Values may be sent and summed in bfloat16 or wider, within the bound.
A program may use at most 128 MiB of HBM per device.

v0:
```python
import jax
import jax.numpy as jnp
from jax import lax
from jax.sharding import Mesh
from jax.sharding import PartitionSpec as P

GX = ("gx_0", "gx_1")
GY = ("gy_0", "gy_1", "gy_2")


def in_blocks(array, dim, devices):
    dims = array.shape
    blocks = array.reshape(*dims[:dim], devices, dims[dim] // devices, *dims[dim + 1 :])
    return jnp.moveaxis(blocks, dim, 0)


def summed_on_arrival(array, axis, dim):
    blocks = in_blocks(array, dim, lax.axis_size(axis))
    arrived = lax.all_to_all(blocks, axis, split_axis=0, concat_axis=0, tiled=True)
    return arrived.sum(axis=0)


def summed_rows(array, axes, dim):
    far, near = axes
    blocks = in_blocks(array, dim, lax.axis_size(far))
    nearer = summed_on_arrival(blocks, near, dim + 1)
    arrived = lax.all_to_all(nearer, far, split_axis=0, concat_axis=0, tiled=True)
    return arrived.sum(axis=0)


def from_everyone(array, axis):
    copies = jnp.broadcast_to(array, (lax.axis_size(axis), *array.shape))
    return lax.all_to_all(copies, axis, split_axis=0, concat_axis=0, tiled=True)


def joined_along(blocks, dim):
    dims = list(blocks.shape[1:])
    dims[dim] *= blocks.shape[0]
    return jnp.moveaxis(blocks, 0, dim).reshape(dims)


def whole_of(array, axes, dim):
    far, near = axes
    leading = from_everyone(array, far)
    blocks = jnp.swapaxes(from_everyone(leading, near), 0, 1)
    return joined_along(blocks.reshape(-1, *array.shape), dim)


def sum_in_order(blocks, axes, order):
    dims = [lax.axis_size(a) for a in axes]
    blocks = blocks.reshape(*dims, *blocks.shape[1:])
    blocks = blocks.transpose(*order, *range(len(axes), blocks.ndim))
    blocks = blocks.reshape(-1, *blocks.shape[len(axes) :])
    for k in order:
        blocks = lax.psum_scatter(blocks, axes[k], scatter_dimension=0, tiled=True)
    return blocks[0]


def scatter_axes(array, axes, order, dim):
    devices = lax.axis_size(axes)
    return sum_in_order(in_blocks(array, dim, devices), axes, order)


def shards(hidden, weight, cotangent):
    tok_rows = hidden.shape[0]
    grad_scale = float(tok_rows * lax.axis_size(GX)) ** (-0.5)
    output_rows = summed_rows(
        lax.dot_general(
            weight, hidden, (((1,), (1,)), ((), ())), preferred_element_type=jnp.float32
        ),
        (("gy_0", "gy_1"), "gy_2"),
        0,
    )
    output = output_rows.T.astype(jnp.bfloat16)
    cotangent_full = whole_of(cotangent, (("gy_0", "gy_1"), "gy_2"), 1)
    hidden_grad = jnp.dot(cotangent_full, weight, preferred_element_type=jnp.float32).astype(
        jnp.bfloat16
    )
    summed = scatter_axes(
        lax.dot_general(
            cotangent_full, hidden, (((0,), (0,)), ((), ())), preferred_element_type=jnp.float32
        ),
        GX,
        (1, 0),
        0,
    )
    weight_grad = summed * grad_scale
    return (output, hidden_grad, weight_grad)


def solution(mesh):
    finer = Mesh(mesh.devices.reshape(2, 8, 2, 4, 2), ("gx_0", "gx_1", "gy_0", "gy_1", "gy_2"))
    placed = (P(GX, GY), P(None, GY), P(GX, GY))
    return jax.shard_map(
        shards,
        mesh=finer,
        in_specs=placed,
        out_specs=(P(GX, GY), P(GX, GY), P(GX, GY)),
        check_vma=False,
    )
```

profile of v0, /device:TPU:1, one launch (start us, length us, event | category | flops | bytes accessed | tf_op | source)
XLA Modules:
  0.0 285.7 jit_solution(610249531185500054)
XLA Ops:
  7.2 0.0 copy-start
  7.2 0.0 reduce-scatter.3.cloned.1.call-start
  7.2 1.2 copy.22
  8.4 0.2 broadcast_in_dim.6
  8.6 31.8 %all_to_all.20 = bf16[8,512,256]{1,2,0:T(8,128)(2,1)S(1)} all-to-all(bf16[8,512,256]{1,2,0:T(8,128)(2,1)S(1)} %broadcast_in_dim.6), channel_id=1, replica_groups=mesh['gx_0'=2,'gx_1'=8,'gy_0'=2,'gy_1'=4,'gy_2'=2] {'gy_0','gy_1'}, dimensions={0} | all-to-all | bytes 4194304 | tf_op jit(solution)/shard_map/all_to_all | solution.py:33
  40.4 0.5 broadcast_in_dim.7
  40.8 9.5 %all_to_all.21 = bf16[2,8,512,256]{2,3,1,0:T(8,128)(2,1)} all-to-all(bf16[2,8,512,256]{2,3,1,0:T(8,128)(2,1)S(1)} %broadcast_in_dim.7), channel_id=1, replica_groups=mesh['gx_0'=2,'gx_1'=8,'gy_0'=2,'gy_1'=4,'gy_2'=2] {'gy_2'}, dimensions={0} | all-to-all | bytes 8388608 | tf_op jit(solution)/shard_map/all_to_all | solution.py:33
  50.4 6.4 %copy.23 = bf16[2,8,512,256]{3,2,0,1:T(8,128)(2,1)} copy(bf16[2,8,512,256]{2,3,1,0:T(8,128)(2,1)} %all_to_all.21) | data formatting | bytes 8388608 | tf_op jit(solution)/shard_map/all_to_all | solution.py:33
  56.8 6.4 %copy.24 = bf16[512,16,256]{0,2,1:T(8,128)(2,1)} copy(bf16[512,16,256]{2,0,1:T(8,128)(2,1)} %bitcast.34) | data formatting | bytes 8388608 | tf_op jit(solution)/shard_map/transpose | solution.py:39
  63.2 0.0 copy-done
  63.2 9.8 %convolution_bitcast_fusion = f32[8,2,256,896]{3,2,0,1:T(8,128)} fusion(bf16[2,8,256,512]{3,2,1,0:T(8,128)(2,1)} %bitcast.36, bf16[512,896]{1,0:T(8,128)(2,1)S(1)} %copy-done), kind=kOutput, calls=%fused_computation.1 | convolution fusion | flops 3758096384 | bytes 19791872 | tf_op jit(solution)/shard_map/dot_general | solution.py:80
  73.0 11.8 %copy.25 = f32[8,2,256,896]{3,2,1,0:T(8,128)} copy(f32[8,2,256,896]{3,2,0,1:T(8,128)} %convolution_bitcast_fusion) | data formatting | bytes 29360128 | tf_op jit(solution)/shard_map/transpose | solution.py:52
  84.8 0.0 reduce-scatter.3.cloned.1.call-update
  84.9 6.9 %fusion.1 = f32[4096,512]{1,0:T(8,128)S(1)} fusion(bf16[4096,896]{1,0:T(8,128)(2,1)} %param.4, bf16[512,896]{1,0:T(8,128)(2,1)S(1)} %copy-done), kind=kOutput, calls=%fused_computation.6 | convolution fusion | flops 3758096384 | bytes 16646144 | tf_op jit(solution)/shard_map/dot_general | solution.py:68
  91.8 1.3 copy.29
  93.2 11.8 %all_to_all.22 = f32[2,8,256,512]{3,2,1,0:T(8,128)} all-to-all(f32[2,8,256,512]{3,2,1,0:T(8,128)S(1)} %bitcast.33), channel_id=1, replica_groups=mesh['gx_0'=2,'gx_1'=8,'gy_0'=2,'gy_1'=4,'gy_2'=2] {'gy_2'}, dimensions={0} | all-to-all | bytes 16777216 | tf_op jit(solution)/shard_map/all_to_all | solution.py:19
  105.0 7.0 %reduce_sum.18 = f32[8,256,512]{2,1,0:T(8,128)} reduce(f32[2,8,256,512]{3,2,1,0:T(8,128)} %all_to_all.22, f32[]{:T(128)} %constant.0.clone.1), dimensions={0}, to_apply=%region_0.0 | reduce | flops 1048576 | bytes 12582916 | tf_op jit(solution)/shard_map/reduce_sum | solution.py:20
  112.0 4.6 %all-to-all-start.1 = ((f32[8,256,512]{2,1,0:T(8,128)}), f32[8,256,512]{2,1,0:T(8,128)}, u32[]{:S(2)}, u32[]{:S(2)}) async-start(f32[8,256,512]{2,1,0:T(8,128)} %reduce_sum.18), calls=%async_computation.1 | async-start | bytes 8388608 | tf_op jit(solution)/shard_map/all_to_all | solution.py:27
  116.6 0.2 reduce-scatter.5.cloned.1.call-start
  116.8 123.2 %reduce-scatter.3.cloned.1.call-done = f32[2,256,896]{2,1,0:T(8,128)} async-done(((f32[16,256,896]{2,1,0:T(8,128)}), f32[2,256,896]{2,1,0:T(8,128)}) %reduce-scatter.3.cloned.1.call-update) | async-done | bytes 1835024 | tf_op jit(solution)/shard_map/reduce_scatter | solution.py:55
  240.0 0.0 reduce-scatter.5.cloned.1.call-update
  240.0 0.0 copy-start.1
  240.0 9.9 %convolution_convert_fusion = bf16[512,896]{1,0:T(8,128)(2,1)} fusion(bf16[512,4096]{0,1:T(8,128)(2,1)} %bitcast.37, bf16[4096,896]{1,0:T(8,128)(2,1)} %param.4), kind=kOutput, calls=%fused_computation.2 | convolution fusion | flops 3758555136 | bytes 12451840 | tf_op jit(solution)/shard_map/dot_general | solution.py:76
  249.9 0.0 all-to-all-done.1
  249.9 2.7 reduce_sum.19
  252.6 0.8 copy.26
  253.4 23.3 %reduce-scatter.5.cloned.1.call-done = f32[1,256,896]{2,1,0:T(8,128)} async-done(((f32[2,256,896]{2,1,0:T(8,128)}), f32[1,256,896]{2,1,0:T(8,128)}) %reduce-scatter.5.cloned.1.call-update) | async-done | bytes 917520 | tf_op jit(solution)/shard_map/reduce_scatter | solution.py:55
  276.7 2.2 multiply_bitcast_fusion
  278.9 0.0 copy-done.1
Async XLA Ops:
  7.2 56.1 %copy-start = (bf16[512,896]{1,0:T(8,128)(2,1)S(1)}, bf16[512,896]{1,0:T(8,128)(2,1)}, u32[]{:S(2)}) copy-start(bf16[512,896]{1,0:T(8,128)(2,1)} %param.3) | copy-start | bytes 2752516
  7.2 232.8 %reduce-scatter.3.cloned.1.call-start = ((), (), s32[]{:S(2)}) async-start(), calls=%async_computation.6 | async-start | bytes 16515072 | tf_op jit(solution)/shard_map/reduce_scatter | solution.py:55
  112.0 137.9 %all-to-all-start.1 = ((f32[8,256,512]{2,1,0:T(8,128)}), f32[8,256,512]{2,1,0:T(8,128)}, u32[]{:S(2)}, u32[]{:S(2)}) async-start(f32[8,256,512]{2,1,0:T(8,128)} %reduce_sum.18), calls=%async_computation.1 | async-start | bytes 8388608 | tf_op jit(solution)/shard_map/all_to_all | solution.py:27
  116.6 160.1 %reduce-scatter.5.cloned.1.call-start = ((), (), s32[]{:S(2)}) async-start(), calls=%async_computation.7 | async-start | bytes 2752512 | tf_op jit(solution)/shard_map/reduce_scatter | solution.py:55
  240.0 38.9 %copy-start.1 = (bf16[512,896]{1,0:T(8,128)(2,1)S(1)}, bf16[512,896]{1,0:T(8,128)(2,1)}, u32[]{:S(2)}) copy-start(bf16[512,896]{1,0:T(8,128)(2,1)} %param.3) | copy-start | bytes 2752516
Sparse Core Ops, SparseCore 0:
  85.0 154.9 reduce-scatter.2
  242.5 34.1 reduce-scatter.4
where the time goes:
time: 286 us
  waiting for transfers between devices  146 us (51%)
  blocking collectives  53.1 us (19%)
  local copies, waits for them, and re-layouts  28.7 us (10%)
  matrix products  26.6 us (9%)
  between operations  14.1 us (5%)
  other arithmetic  11.9 us (4%)
  starting transfers between devices  4.83 us (2%)
    reduce_scatter x2, waiting for transfers between devices, sum_in_order(): blocks = lax.psum_scatter(blocks, axes[k], scatter_dimension=0, tiled=True)  146 us
    all_to_all x2, blocking collectives, from_everyone(): return lax.all_to_all(copies, axis, split_axis=0, concat_axis=0, tiled=True)  41.3 us
    transpose x1, local copies, waits for them, and re-layouts, sum_in_order(): blocks = blocks.transpose(*order, *range(len(axes), blocks.ndim))  11.8 us
    all_to_all x1, blocking collectives, summed_on_arrival(): lax.all_to_all(blocks, axis, split_axis=0, concat_axis=0, tiled=True)  11.8 us
    dot_general x1, matrix products, shards(): jnp.dot(cotangent_full, weight, preferred_element_type=jnp.float32)  9.85 us
    dot_general x1, matrix products, shards(): lax.dot_general(cotangent_full, hidden, (((0,), (0,)), ((), ())), preferr...  9.79 us
    reduce_sum x1, other arithmetic, summed_on_arrival(): return arrived.sum(axis=0)  7.03 us
    dot_general x1, matrix products, shards(): lax.dot_general(weight, hidden, (((1,), (1,)), ((), ())), preferred_eleme...  6.95 us
  transfers between devices with their start and end apart: 3, of which 2 were waited for; matrix products, arithmetic and copies ran while one was open for 10% of the time, Pallas kernels for 0%

commit v1 on v0

v1 whole, which is shorter than its diff:
```python
import functools

import jax
import jax.numpy as jnp
from jax import lax
from jax.experimental import pallas as pl
from jax.experimental.pallas import tpu as pltpu
from jax.sharding import PartitionSpec as P

MESH = pl.DeviceIdType.MESH
F32 = jnp.float32
BF16 = jnp.bfloat16
NX, NZ = 4, 8
HCH = 4
WCH = 4


def zigzag(i, top):
    odd = lax.rem(i, 2)
    return top + (1 - odd) * (i // 2) - odd * ((i + 1) // 2)


def kernel(
    scale,
    hidden,
    weight,
    cotangent,
    output,
    hidden_grad,
    weight_grad,
    w,
    hid,
    hrel,
    cot,
    o_send,
    o_sum,
    xh,
    xf,
    yb,
    part,
    zb,
    acc,
    hgb,
    outb,
    load_sem,
    store_sem,
    cy_s,
    cy_r,
    cx_s,
    cx_r,
    cd_s,
    cd_r,
    h_s,
    h_r,
    o_s,
    o_r,
    xo_s,
    xo_r,
    yo_s,
    yo_r,
    z_s,
    z_r,
):
    gx = lax.axis_index("gx")
    gy = lax.axis_index("gy")
    y_hi, z = gx // NZ, lax.rem(gx, NZ)
    c = lax.rem(gy, 2)
    x = lax.rem(gy // 2, NX)
    y_lo = gy // (2 * NX)
    tok, ff = hid.shape[1], hid.shape[2]
    feat = cot.shape[2]
    half = tok // 2
    rows = feat // 2

    def dev(yh, yl, xx, zz, cc):
        return (yh * NZ + zz, (yl * NX + xx) * 2 + cc)

    right, left = lax.rem(x + 1, NX), lax.rem(x + NX - 1, NX)
    across = lax.rem(x + 2, NX)
    core = dev(y_hi, y_lo, x, z, 1 - c)
    near = dev(y_hi, 1 - y_lo, x, z, c)
    far = dev(1 - y_hi, 1 - y_lo, x, z, c)
    first = dev(lax.rem(y_hi + c, 2), 1 - y_lo, x, z, c)
    second = dev(lax.rem(y_hi + 1 - c, 2), 1 - y_lo, x, z, c)
    x_dev = (dev(y_hi, y_lo, right, z, c), dev(y_hi, y_lo, left, z, c))
    z_dev = (
        dev(y_hi, y_lo, x, lax.rem(z + 1, NZ), c),
        dev(y_hi, y_lo, x, lax.rem(z + NZ - 1, NZ), c),
    )

    def rc(src, dst, ss, rs, to):
        return pltpu.make_async_remote_copy(
            src_ref=src, dst_ref=dst, send_sem=ss, recv_sem=rs, device_id=to, device_id_type=MESH
        )

    sent = []

    def go(copy):
        copy.start()
        sent.append(copy)

    base = (y_lo * NX * 2, (1 - y_lo) * NX * 2, 16)

    def slot(kind, xx):
        return cot.at[base[kind] + xx * 2 + c]

    mine = slot(0, x)
    ld_cot = pltpu.make_async_copy(cotangent, mine, load_sem.at[0])
    ld_hid = pltpu.make_async_copy(hidden, hid.at[0], load_sem.at[1])
    ld_cot.start()
    ld_hid.start()
    wrows = w.shape[0] // WCH
    ld_w = [
        pltpu.make_async_copy(
            weight.at[pl.ds(i * wrows, wrows)], w.at[pl.ds(i * wrows, wrows)], load_sem.at[2 + i]
        )
        for i in range(WCH)
    ]
    for copy in ld_w:
        copy.start()

    barrier = pltpu.get_barrier_semaphore()
    peers = (core, near, far, *x_dev, *z_dev)
    for peer in peers:
        pl.semaphore_signal(barrier, inc=1, device_id=peer, device_id_type=MESH)
    pl.semaphore_wait(barrier, len(peers))

    def xs_full(kind, d):
        return rc(slot(kind, x), slot(kind, x), cx_s.at[kind, d], cx_r.at[kind, d], x_dev[d])

    def xs_half(kind, d):
        src = slot(kind, (left, right)[d]).at[pl.ds(d * half, half)]
        return rc(src, src, cx_s.at[kind, 2 + d], cx_r.at[kind, 2 + d], x_dev[d])

    def from_full(kind, d):
        ref = slot(kind, (left, right)[d])
        return rc(ref, ref, cx_s.at[kind, d], cx_r.at[kind, d], x_dev[d])

    def from_half(kind, d):
        ref = slot(kind, across).at[pl.ds(d * half, half)]
        return rc(ref, ref, cx_s.at[kind, 2 + d], cx_r.at[kind, 2 + d], x_dev[d])

    def to_core(kind, j):
        ref = slot(kind, (x, left, right, across)[j])
        return rc(ref, ref, cd_s.at[kind, j], cd_r.at[kind, j], core)

    def from_core(kind, j):
        ref = cot.at[base[kind] + (x, left, right, across)[j] * 2 + 1 - c]
        return rc(ref, ref, cd_s.at[kind, j], cd_r.at[kind, j], core)

    def spread(kind):
        go(xs_full(kind, 0))
        go(xs_full(kind, 1))
        go(to_core(kind, 0))

    def relay(kind):
        for d in range(2):
            from_full(kind, d).wait_recv()
            go(xs_half(kind, d))
        go(to_core(kind, 1))
        go(to_core(kind, 2))

    def finish(kind):
        for d in range(2):
            from_half(kind, d).wait_recv()
        go(to_core(kind, 3))

    ld_cot.wait()
    near_slot, far_slot = slot(1, x), slot(2, x)
    go(rc(mine, near_slot_of(cot, y_lo, x, c), cy_s.at[0], cy_r.at[0], near))
    middle = y_hi != y_lo

    @pl.when(middle)
    def _():
        rc(mine, far_slot, cy_s.at[1], cy_r.at[1], far).start()

    spread(0)

    hrows = tok // HCH

    def hpiece(ref, i):
        return ref.at[pl.ds(i * hrows, hrows)]

    ld_hid.wait()
    for i in range(HCH):
        go(rc(hpiece(hid.at[0], i), hpiece(hrel, i), h_s.at[0, i], h_r.at[0, i], first))

    def hrelay(i):
        ref = hpiece(hrel, i)
        rc(ref, ref, h_s.at[0, i], h_r.at[0, i], first).wait_recv()
        go(rc(ref, hpiece(hid.at[1], i), h_s.at[1, i], h_r.at[1, i], second))

    def out_part(t, cc):
        yp = lax.rem(y_lo + 1 + lax.rem(t, 2), 2)
        g = (yp * NX + lax.rem(x + zigzag(t // 2, 2), NX)) * 2 + cc
        wg = w[pl.ds(pl.multiple_of(g * feat, feat), feat), :]
        return lax.dot_general(hid[0], wg, (((1,), (1,)), ((), ())), preferred_element_type=F32)

    def o_copy(t):
        return rc(o_send.at[t], o_sum.at[t], o_s.at[t], o_r.at[t], core)

    for copy in ld_w:
        copy.wait()

    def send_out(t, _):
        o_send[t] = out_part(t, 1 - c)
        o_copy(t).start()
        return 0

    lax.fori_loop(0, 4, send_out, 0)

    rc(near_slot, near_slot, cy_s.at[0], cy_r.at[0], near).wait_recv()

    @pl.when(jnp.logical_not(middle))
    def _():
        rc(near_slot, far_slot, cy_s.at[1], cy_r.at[1], far).start()

    spread(1)
    hrelay(0)
    relay(0)
    lax.fori_loop(4, 8, send_out, 0)
    hrelay(1)
    rc(far_slot, far_slot, cy_s.at[1], cy_r.at[1], far).wait_recv()
    spread(2)
    relay(1)
    hrelay(2)

    def add_out(t, _):
        o_copy(t).wait_recv()
        o_sum[t] = o_sum[t] + out_part(t, c)
        return 0

    lax.fori_loop(0, 8, add_out, 0)
    finish(0)
    hrelay(3)
    relay(2)
    finish(1)

    def xo_half(d, q):
        src = o_sum.at[q].at[pl.ds(d * half, half)]
        return rc(src, xh.at[d, q], xo_s.at[0, d, q], xo_r.at[0, d, q], x_dev[d])

    def xo_full(d, q):
        return rc(o_sum.at[2 + 2 * d + q], xf.at[d, q], xo_s.at[1, d, q], xo_r.at[1, d, q], x_dev[d])

    finish(2)
    for q in range(2):
        for d in range(2):
            go(xo_half(d, q))
    for kind in range(3):
        for j in range(4):
            from_core(kind, j).wait_recv()
    for i in range(HCH):
        ref = hpiece(hid.at[1], i)
        rc(ref, ref, h_s.at[1, i], h_r.at[1, i], second).wait_recv()

    def w_part(i, _):
        zz = lax.rem(z + zigzag(i, 4), NZ)
        dims = (((0,), (0,)), ((), ()))
        part[i] = lax.dot_general(
            cot[y_hi * NZ + zz], hid[0], dims, preferred_element_type=F32
        ) + lax.dot_general(cot[16 + zz], hid[1], dims, preferred_element_type=F32)
        return 0

    index_of = {4: 0, 3: 1, 5: 2, 2: 3, 6: 4, 1: 5, 7: 6, 0: 7}

    def z_part(d, m):
        k = 4 - (m + 1) // 2
        piece = (m + d) % 2
        return part.at[index_of[(k if d == 0 else -k) % NZ]].at[pl.ds(piece * rows, rows)]

    def z_copy(d, m):
        src = z_part(d, m) if m < 2 else zb.at[d, m - 2]
        return rc(src, zb.at[d, m], z_s.at[d, m], z_r.at[d, m], z_dev[d])

    def z_step(m):
        for d in range(2):
            z_copy(d, m - 2).wait_recv()
            zb[d, m - 2] = zb[d, m - 2] + z_part(d, m)[...]
            go(z_copy(d, m))

    lax.fori_loop(0, 3, w_part, 0)
    for m in range(2):
        for d in range(2):
            go(z_copy(d, m))
    lax.fori_loop(3, 8, w_part, 0)

    def h_part(g, _):
        acc[...] = acc[...] + jnp.dot(
            cot[g], w[pl.ds(pl.multiple_of(g * feat, feat), feat), :], preferred_element_type=F32
        )
        return 0

    acc[...] = jnp.dot(cot[0], w[pl.ds(0, feat), :], preferred_element_type=F32)
    lax.fori_loop(1, 16, h_part, 0)
    hgb[...] = acc[...].astype(BF16)
    st_hg = pltpu.make_async_copy(hgb, hidden_grad, store_sem.at[0])
    st_hg.start()

    def xo_add(q):
        xo_half(0, q).wait_recv()
        o_sum[2 + q, pl.ds(0, half)] = o_sum[2 + q, pl.ds(0, half)] + xh[0, q]
        go(xo_full(0, q))
        xo_half(1, q).wait_recv()
        o_sum[4 + q, pl.ds(half, half)] = o_sum[4 + q, pl.ds(half, half)] + xh[1, q]
        go(xo_full(1, q))

    def xo_end(q):
        for d in range(2):
            xo_full(d, q).wait_recv()
        o_sum[6 + q] = o_sum[6 + q] + xf[0, q] + xf[1, q]

    yo = rc(o_sum.at[6], yb, yo_s.at[0], yo_r.at[0], near)
    z_step(2)
    xo_add(0)
    xo_add(1)
    z_step(3)
    z_step(4)
    xo_end(0)
    go(yo)
    z_step(5)
    xo_end(1)
    z_step(6)
    yo.wait_recv()
    outb[...] = (o_sum[7] + yb[...]).astype(BF16)
    st_out = pltpu.make_async_copy(outb, output, store_sem.at[1])
    st_out.start()

    z_copy(0, 5).wait_recv()
    z_copy(1, 5).wait_recv()
    z_copy(0, 6).wait_recv()
    z_copy(1, 6).wait_recv()
    part[7, pl.ds(0, rows)] = (part[7, pl.ds(0, rows)] + zb[0, 6] + zb[1, 5]) * scale
    part[7, pl.ds(rows, rows)] = (part[7, pl.ds(rows, rows)] + zb[0, 5] + zb[1, 6]) * scale
    st_wg = pltpu.make_async_copy(part.at[7], weight_grad, store_sem.at[2])
    st_wg.start()

    rc(mine, far_slot, cy_s.at[1], cy_r.at[1], far).wait_send()

    def sent_out(t, _):
        o_copy(t).wait_send()
        return 0

    lax.fori_loop(0, 8, sent_out, 0)
    for copy in sent:
        copy.wait_send()
    st_hg.wait()
    st_out.wait()
    st_wg.wait()


def near_slot_of(cot, y_lo, x, c):
    return cot.at[y_lo * NX * 2 + x * 2 + c]


def shards(hidden, weight, cotangent):
    tok, ff = hidden.shape
    d_all = weight.shape[0]
    feat = cotangent.shape[1]
    scale = float(tok * lax.axis_size("gx")) ** (-0.5)
    any_space = pl.BlockSpec(memory_space=pl.ANY)
    sem = pltpu.SemaphoreType.DMA
    v = pltpu.VMEM
    return pl.pallas_call(
        functools.partial(kernel, scale),
        out_shape=(
            jax.ShapeDtypeStruct((tok, feat), BF16),
            jax.ShapeDtypeStruct((tok, ff), BF16),
            jax.ShapeDtypeStruct((feat, ff), F32),
        ),
        in_specs=[any_space] * 3,
        out_specs=(any_space,) * 3,
        scratch_shapes=[
            v((d_all, ff), BF16),
            v((2, tok, ff), BF16),
            v((tok, ff), BF16),
            v((24, tok, feat), BF16),
            v((8, tok, feat), F32),
            v((8, tok, feat), F32),
            v((2, 2, tok // 2, feat), F32),
            v((2, 2, tok, feat), F32),
            v((tok, feat), F32),
            v((8, feat, ff), F32),
            v((2, 7, feat // 2, ff), F32),
            v((tok, ff), F32),
            v((tok, ff), BF16),
            v((tok, feat), BF16),
            sem((2 + WCH,)),
            sem((3,)),
            sem((2,)),
            sem((2,)),
            sem((3, 4)),
            sem((3, 4)),
            sem((3, 4)),
            sem((3, 4)),
            sem((2, HCH)),
            sem((2, HCH)),
            sem((8,)),
            sem((8,)),
            sem((2, 2, 2)),
            sem((2, 2, 2)),
            sem((1,)),
            sem((1,)),
            sem((2, 7)),
            sem((2, 7)),
        ],
        compiler_params=pltpu.CompilerParams(
            collective_id=0, has_side_effects=True, vmem_limit_bytes=62 * 1024 * 1024
        ),
    )(hidden, weight, cotangent)


def solution(mesh):
    placed = (P("gx", "gy"), P(None, "gy"), P("gx", "gy"))
    return jax.shard_map(
        shards,
        mesh=mesh,
        in_specs=placed,
        out_specs=(P("gx", "gy"), P("gx", "gy"), P("gx", "gy")),
        check_vma=False,
    )
```

time: 286 us -> 122 us (0.43)
  waiting for transfers between devices: 146 us -> 0 us
  Pallas kernels: 0 us -> 115 us
  blocking collectives: 53.1 us -> 0 us
  matrix products: 26.6 us -> 0 us
  local copies, waits for them, and re-layouts: 28.7 us -> 6 us
  between operations: 14.1 us -> 0.64 us
  other arithmetic: 11.9 us -> 0 us
  starting transfers between devices: 4.83 us -> 0 us
    reduce_scatter x2 -> x0, waiting for transfers between devices: 146 us -> none  [sum_in_order(): blocks = lax.psum_scatter(blocks, axes[k], scatter_dimension=0, tiled=True)]
    pallas_call x0 -> x1, Pallas kernels: none -> 115 us  [shards(): pl.pallas_call(functools.partial(kernel, scale), out_shape=(jax.ShapeDtyp...]
    all_to_all x3 -> x0, blocking collectives: 53.1 us -> none  [the longest x2 41.3 us: from_everyone(): return lax.all_to_all(copies, axis, split_axis=0, concat_axis=0, tiled=True)]
    dot_general x3 -> x0, matrix products: 26.6 us -> none  [the longest x1 9.85 us: shards(): jnp.dot(cotangent_full, weight, preferred_element_type=jnp.float32)]
    transpose x2 -> x0, local copies, waits for them, and re-layouts: 18.2 us -> none  [the longest x1 11.8 us: sum_in_order(): blocks = blocks.transpose(*order, *range(len(axes), blocks.ndim))]
    reduce_sum x2 -> x0, other arithmetic: 9.72 us -> none  [the longest x1 7.03 us: summed_on_arrival(): return arrived.sum(axis=0)]
    all_to_all x1 -> x0, local copies, waits for them, and re-layouts: 6.43 us -> none  [from_everyone(): return lax.all_to_all(copies, axis, split_axis=0, concat_axis=0, tiled=True)]
    all_to_all x1 -> x0, starting transfers between devices: 4.57 us -> none  [summed_rows(): lax.all_to_all(nearer, far, split_axis=0, concat_axis=0, tiled=True)]
  transfers between devices with their start and end apart: 3 -> 0, of which waited for: 2 -> 0; matrix products, arithmetic and copies ran while one was open for 10% -> 0% of each run, Pallas kernels for 0% -> 0%
where the time goes in v1:
time: 122 us; the launch traced here: 121 us
  Pallas kernels  115 us (94%)
  local copies, waits for them, and re-layouts  6 us (5%)
    pallas_call x1, Pallas kernels, shards(): pl.pallas_call(functools.partial(kernel, scale), out_shape=(jax.ShapeDtyp...  115 us
    unnamed x3, local copies, waits for them, and re-layouts  6 us

profile of v1, /device:TPU:1, one launch (start us, length us, event | category | flops | bytes accessed | tf_op | source)
XLA Modules:
  0.0 121.4 jit_solution(146821675305918993)
XLA Ops:
  0.6 114.8 %shard_map.58 = (bf16[512,256]{1,0:T(8,128)(2,1)}, bf16[512,896]{1,0:T(8,128)(2,1)}, f32[256,896]{1,0:T(8,128)}) custom-call(bf16[512,896]{1,0:T(8,128)(2,1)} %hidden.1, bf16[4096,896]{1,0:T(8,128)(2,1)} %weight.1, bf16[512,256]{1,0:T(8,128)(2,1)} %cotangent.1), custom_call_target="tpu_custom_call" | custom-call | tf_op jit(solution)/shard_map/pallas_call | solution.py:364
  115.4 1.7 %copy.9 = bf16[512,256]{1,0:T(8,128)(2,1)} copy(bf16[512,256]{1,0:T(8,128)(2,1)} %get-tuple-element.6) | data formatting | bytes 524288
  117.1 2.2 %copy.10 = bf16[512,896]{1,0:T(8,128)(2,1)} copy(bf16[512,896]{1,0:T(8,128)(2,1)} %get-tuple-element.7) | data formatting | bytes 1835008
  119.3 2.2 %copy.11 = f32[256,896]{1,0:T(8,128)} copy(f32[256,896]{1,0:T(8,128)} %get-tuple-element.8) | data formatting | bytes 1835008

commit v2 on v1

--- a/solution.py
+++ b/solution.py
@@ -13,6 +13,7 @@
 NX, NZ = 4, 8
 HCH = 4
 WCH = 4
+ZR = 16
 
 
 def zigzag(i, top):
@@ -38,6 +39,7 @@
     xf,
     yb,
     part,
+    zs,
     zb,
     acc,
     hgb,
@@ -95,16 +97,19 @@
 
     sent = []
 
-    def go(copy):
-        copy.start()
-        sent.append(copy)
-
-    base = (y_lo * NX * 2, (1 - y_lo) * NX * 2, 16)
+    def go(make, *where):
+        make(*where).start()
+        sent.append((make, where))
+
+    base = (y_hi * NX * 2, (1 - y_hi) * NX * 2, 16)
+    middle = lax.rem(y_hi + y_lo, 2)
 
     def slot(kind, xx):
         return cot.at[base[kind] + xx * 2 + c]
 
-    mine = slot(0, x)
+    mine = cot.at[y_lo * NX * 2 + x * 2 + c]
+    near_slot = cot.at[(1 - y_lo) * NX * 2 + x * 2 + c]
+    far_slot = slot(2, x)
     ld_cot = pltpu.make_async_copy(cotangent, mine, load_sem.at[0])
     ld_hid = pltpu.make_async_copy(hidden, hid.at[0], load_sem.at[1])
     ld_cot.start()
@@ -148,47 +153,68 @@
         ref = cot.at[base[kind] + (x, left, right, across)[j] * 2 + 1 - c]
         return rc(ref, ref, cd_s.at[kind, j], cd_r.at[kind, j], core)
 
-    def spread(kind):
-        go(xs_full(kind, 0))
-        go(xs_full(kind, 1))
-        go(to_core(kind, 0))
+    def to_near():
+        return rc(mine, mine, cy_s.at[0], cy_r.at[0], near)
+
+    def from_near():
+        return rc(near_slot, near_slot, cy_s.at[0], cy_r.at[0], near)
+
+    def to_far(src):
+        return rc(src, far_slot, cy_s.at[1], cy_r.at[1], far)
+
+    def spread_own(outer):
+        kind = 0 if outer else 1
+        xs_full(kind, 0).start()
+        xs_full(kind, 1).start()
+        to_core(kind, 0).start()
 
     def relay(kind):
         for d in range(2):
             from_full(kind, d).wait_recv()
-            go(xs_half(kind, d))
-        go(to_core(kind, 1))
-        go(to_core(kind, 2))
+            xs_half(kind, d).start()
+        to_core(kind, 1).start()
+        to_core(kind, 2).start()
+
+    def relayed(kind):
+        for d in range(2):
+            sent.append((xs_half, (kind, d)))
+            sent.append((to_core, (kind, 1 + d)))
 
     def finish(kind):
         for d in range(2):
             from_half(kind, d).wait_recv()
-        go(to_core(kind, 3))
+        go(to_core, kind, 3)
+
+    def when_outer(run):
+        pl.when(middle == 0)(run)
+
+    def when_middle(run):
+        pl.when(middle == 1)(run)
 
     ld_cot.wait()
-    near_slot, far_slot = slot(1, x), slot(2, x)
-    go(rc(mine, near_slot_of(cot, y_lo, x, c), cy_s.at[0], cy_r.at[0], near))
-    middle = y_hi != y_lo
-
-    @pl.when(middle)
-    def _():
-        rc(mine, far_slot, cy_s.at[1], cy_r.at[1], far).start()
-
-    spread(0)
+    go(to_near)
+    when_middle(lambda: to_far(mine).start())
+    when_outer(lambda: spread_own(True))
+    when_middle(lambda: spread_own(False))
 
     hrows = tok // HCH
 
     def hpiece(ref, i):
         return ref.at[pl.ds(i * hrows, hrows)]
 
+    def h_first(i):
+        return rc(hpiece(hid.at[0], i), hpiece(hrel, i), h_s.at[0, i], h_r.at[0, i], first)
+
+    def h_second(i):
+        return rc(hpiece(hrel, i), hpiece(hid.at[1], i), h_s.at[1, i], h_r.at[1, i], second)
+
+    def hrelay(i):
+        h_first(i).wait_recv()
+        go(h_second, i)
+
     ld_hid.wait()
-    for i in range(HCH):
-        go(rc(hpiece(hid.at[0], i), hpiece(hrel, i), h_s.at[0, i], h_r.at[0, i], first))
-
-    def hrelay(i):
-        ref = hpiece(hrel, i)
-        rc(ref, ref, h_s.at[0, i], h_r.at[0, i], first).wait_recv()
-        go(rc(ref, hpiece(hid.at[1], i), h_s.at[1, i], h_r.at[1, i], second))
+    go(h_first, 0)
+    go(h_first, 1)
 
     def out_part(t, cc):
         yp = lax.rem(y_lo + 1 + lax.rem(t, 2), 2)
@@ -199,42 +225,61 @@
     def o_copy(t):
         return rc(o_send.at[t], o_sum.at[t], o_s.at[t], o_r.at[t], core)
 
-    for copy in ld_w:
-        copy.wait()
-
     def send_out(t, _):
         o_send[t] = out_part(t, 1 - c)
         o_copy(t).start()
         return 0
 
-    lax.fori_loop(0, 4, send_out, 0)
-
-    rc(near_slot, near_slot, cy_s.at[0], cy_r.at[0], near).wait_recv()
-
-    @pl.when(jnp.logical_not(middle))
-    def _():
-        rc(near_slot, far_slot, cy_s.at[1], cy_r.at[1], far).start()
-
-    spread(1)
-    hrelay(0)
-    relay(0)
-    lax.fori_loop(4, 8, send_out, 0)
-    hrelay(1)
-    rc(far_slot, far_slot, cy_s.at[1], cy_r.at[1], far).wait_recv()
-    spread(2)
-    relay(1)
-    hrelay(2)
-
     def add_out(t, _):
         o_copy(t).wait_recv()
         o_sum[t] = o_sum[t] + out_part(t, c)
         return 0
 
-    lax.fori_loop(0, 8, add_out, 0)
+    for copy in ld_w:
+        copy.wait()
+    lax.fori_loop(0, 8, send_out, 0)
+
+    from_near().wait_recv()
+
+    def outer_near():
+        to_far(near_slot).start()
+        spread_own(False)
+        relay(0)
+
+    def middle_near():
+        spread_own(True)
+        to_far(far_slot).wait_recv()
+        xs_full(2, 0).start()
+        xs_full(2, 1).start()
+        to_core(2, 0).start()
+
+    when_outer(outer_near)
+    when_middle(middle_near)
+    for kind in range(3):
+        sent.extend([(xs_full, (kind, 0)), (xs_full, (kind, 1)), (to_core, (kind, 0))])
+        relayed(kind)
+
+    hrelay(0)
+    go(h_first, 2)
+    lax.fori_loop(0, 2, add_out, 0)
+    hrelay(1)
+    go(h_first, 3)
+
+    def outer_far():
+        to_far(far_slot).wait_recv()
+        xs_full(2, 0).start()
+        xs_full(2, 1).start()
+        to_core(2, 0).start()
+
+    when_outer(outer_far)
+    when_middle(lambda: relay(0))
+    lax.fori_loop(2, 6, add_out, 0)
+    hrelay(2)
+    relay(2)
+    lax.fori_loop(6, 8, add_out, 0)
     finish(0)
     hrelay(3)
-    relay(2)
-    finish(1)
+    relay(1)
 
     def xo_half(d, q):
         src = o_sum.at[q].at[pl.ds(d * half, half)]
@@ -243,16 +288,15 @@
     def xo_full(d, q):
         return rc(o_sum.at[2 + 2 * d + q], xf.at[d, q], xo_s.at[1, d, q], xo_r.at[1, d, q], x_dev[d])
 
-    finish(2)
     for q in range(2):
         for d in range(2):
-            go(xo_half(d, q))
-    for kind in range(3):
+            go(xo_half, d, q)
+    finish(2)
+    for kind in (0, 2):
         for j in range(4):
             from_core(kind, j).wait_recv()
     for i in range(HCH):
-        ref = hpiece(hid.at[1], i)
-        rc(ref, ref, h_s.at[1, i], h_r.at[1, i], second).wait_recv()
+        h_second(i).wait_recv()
 
     def w_part(i, _):
         zz = lax.rem(z + zigzag(i, 4), NZ)
@@ -264,26 +308,82 @@
 
     index_of = {4: 0, 3: 1, 5: 2, 2: 3, 6: 4, 1: 5, 7: 6, 0: 7}
 
-    def z_part(d, m):
+    def z_rows(d, m):
         k = 4 - (m + 1) // 2
-        piece = (m + d) % 2
-        return part.at[index_of[(k if d == 0 else -k) % NZ]].at[pl.ds(piece * rows, rows)]
+        return index_of[(k if d == 0 else -k) % NZ], ((m + d) % 2) * rows
 
     def z_copy(d, m):
-        src = z_part(d, m) if m < 2 else zb.at[d, m - 2]
+        src = zs.at[d, m] if m < 2 else zb.at[d, m - 2]
         return rc(src, zb.at[d, m], z_s.at[d, m], z_r.at[d, m], z_dev[d])
 
+    def coded(v):
+        high = v.astype(BF16)
+        near_v = high.astype(F32)
+        fit = jnp.abs(near_v) > 1e-36
+        ratio = jnp.where(fit, (v - near_v) / jnp.where(fit, near_v, 1.0), 0.0)
+        return high, jnp.clip(jnp.round(ratio * 2560.0), -10.0, 10.0)
+
+    def take(ref, r):
+        low = ref[pl.ds(rows + r, ZR)].astype(F32)
+        q0 = jnp.round(low * (1.0 / 21.0))
+        q1 = low - 21.0 * q0
+        h0 = ref[pl.ds(r, ZR)].astype(F32)
+        h1 = ref[pl.ds(rows // 2 + r, ZR)].astype(F32)
+        return h0 + h0 * (q0 * (1.0 / 2560.0)), h1 + h1 * (q1 * (1.0 / 2560.0))
+
+    def put(ref, r, v0, v1):
+        h0, q0 = coded(v0)
+        h1, q1 = coded(v1)
+        ref[pl.ds(r, ZR)] = h0
+        ref[pl.ds(rows // 2 + r, ZR)] = h1
+        ref[pl.ds(rows + r, ZR)] = (q0 * 21.0 + q1).astype(BF16)
+
+    def in_rows(run):
+        def body(i, _):
+            run(pl.multiple_of(i * ZR, ZR))
+            return 0
+
+        lax.fori_loop(0, rows // 2 // ZR, body, 0)
+
+    def part_rows(i, start, r):
+        at = pl.ds(start + r, ZR), pl.ds(start + rows // 2 + r, ZR)
+        return part[i, at[0]], part[i, at[1]]
+
+    def z_first(d, m):
+        i, start = z_rows(d, m)
+
+        def run(r):
+            put(zs.at[d, m], r, *part_rows(i, start, r))
+
+        in_rows(run)
+        go(z_copy, d, m)
+
+    def z_one(d, m):
+        z_copy(d, m - 2).wait_recv()
+        i, start = z_rows(d, m)
+
+        def run(r):
+            p0, p1 = part_rows(i, start, r)
+            s0, s1 = take(zb.at[d, m - 2], r)
+            put(zb.at[d, m - 2], r, s0 + p0, s1 + p1)
+
+        in_rows(run)
+        go(z_copy, d, m)
+
     def z_step(m):
-        for d in range(2):
-            z_copy(d, m - 2).wait_recv()
-            zb[d, m - 2] = zb[d, m - 2] + z_part(d, m)[...]
-            go(z_copy(d, m))
-
-    lax.fori_loop(0, 3, w_part, 0)
-    for m in range(2):
-        for d in range(2):
-            go(z_copy(d, m))
+        z_one(0, m)
+        z_one(1, m)
+
+    lax.fori_loop(0, 1, w_part, 0)
+    z_first(0, 0)
+    z_first(1, 0)
+    lax.fori_loop(1, 3, w_part, 0)
+    z_first(0, 1)
+    z_first(1, 1)
     lax.fori_loop(3, 8, w_part, 0)
+    finish(1)
+    for j in range(4):
+        from_core(1, j).wait_recv()
 
     def h_part(g, _):
         acc[...] = acc[...] + jnp.dot(
@@ -300,17 +400,19 @@
     def xo_add(q):
         xo_half(0, q).wait_recv()
         o_sum[2 + q, pl.ds(0, half)] = o_sum[2 + q, pl.ds(0, half)] + xh[0, q]
-        go(xo_full(0, q))
+        go(xo_full, 0, q)
         xo_half(1, q).wait_recv()
         o_sum[4 + q, pl.ds(half, half)] = o_sum[4 + q, pl.ds(half, half)] + xh[1, q]
-        go(xo_full(1, q))
+        go(xo_full, 1, q)
 
     def xo_end(q):
         for d in range(2):
             xo_full(d, q).wait_recv()
         o_sum[6 + q] = o_sum[6 + q] + xf[0, q] + xf[1, q]
 
-    yo = rc(o_sum.at[6], yb, yo_s.at[0], yo_r.at[0], near)
+    def yo():
+        return rc(o_sum.at[6], yb, yo_s.at[0], yo_r.at[0], near)
+
     z_step(2)
     xo_add(0)
     xo_add(1)
@@ -321,36 +423,41 @@
     z_step(5)
     xo_end(1)
     z_step(6)
-    yo.wait_recv()
+    yo().wait_recv()
     outb[...] = (o_sum[7] + yb[...]).astype(BF16)
     st_out = pltpu.make_async_copy(outb, output, store_sem.at[1])
     st_out.start()
 
-    z_copy(0, 5).wait_recv()
-    z_copy(1, 5).wait_recv()
-    z_copy(0, 6).wait_recv()
-    z_copy(1, 6).wait_recv()
-    part[7, pl.ds(0, rows)] = (part[7, pl.ds(0, rows)] + zb[0, 6] + zb[1, 5]) * scale
-    part[7, pl.ds(rows, rows)] = (part[7, pl.ds(rows, rows)] + zb[0, 5] + zb[1, 6]) * scale
+    def z_end(start, m0, m1):
+        z_copy(0, m0).wait_recv()
+        z_copy(1, m1).wait_recv()
+
+        def run(r):
+            p0, p1 = part_rows(7, start, r)
+            s0, s1 = take(zb.at[0, m0], r)
+            t0, t1 = take(zb.at[1, m1], r)
+            part[7, pl.ds(start + r, ZR)] = (p0 + s0 + t0) * scale
+            part[7, pl.ds(start + rows // 2 + r, ZR)] = (p1 + s1 + t1) * scale
+
+        in_rows(run)
+
+    z_end(0, 6, 5)
+    z_end(rows, 5, 6)
     st_wg = pltpu.make_async_copy(part.at[7], weight_grad, store_sem.at[2])
     st_wg.start()
 
-    rc(mine, far_slot, cy_s.at[1], cy_r.at[1], far).wait_send()
+    to_far(mine).wait_send()
 
     def sent_out(t, _):
         o_copy(t).wait_send()
         return 0
 
     lax.fori_loop(0, 8, sent_out, 0)
-    for copy in sent:
-        copy.wait_send()
+    for make, where in sent:
+        make(*where).wait_send()
     st_hg.wait()
     st_out.wait()
     st_wg.wait()
-
-
-def near_slot_of(cot, y_lo, x, c):
-    return cot.at[y_lo * NX * 2 + x * 2 + c]
 
 
 def shards(hidden, weight, cotangent):
@@ -381,7 +488,8 @@
             v((2, 2, tok, feat), F32),
             v((tok, feat), F32),
             v((8, feat, ff), F32),
-            v((2, 7, feat // 2, ff), F32),
+            v((2, 2, feat * 3 // 4, ff), BF16),
+            v((2, 7, feat * 3 // 4, ff), BF16),
             v((tok, ff), F32),
             v((tok, ff), BF16),
             v((tok, feat), BF16),

time: 122 us -> 103 us (0.84)
  Pallas kernels: 115 us -> 96.5 us
    pallas_call x1, Pallas kernels: 115 us -> 96.5 us  [shards(): pl.pallas_call(functools.partial(kernel, scale), out_shape=(jax.ShapeDtyp...]
where the time goes in v2:
time: 103 us
  Pallas kernels  96.5 us (94%)
  local copies, waits for them, and re-layouts  6 us (6%)
    pallas_call x1, Pallas kernels, shards(): pl.pallas_call(functools.partial(kernel, scale), out_shape=(jax.ShapeDtyp...  96.5 us
    unnamed x3, local copies, waits for them, and re-layouts  6 us

profile of v2, /device:TPU:1, one launch (start us, length us, event | category | flops | bytes accessed | tf_op | source)
XLA Modules:
  0.0 103.1 jit_solution(12506754546189912709)
XLA Ops:
  0.6 96.5 %shard_map.58 = (bf16[512,256]{1,0:T(8,128)(2,1)}, bf16[512,896]{1,0:T(8,128)(2,1)}, f32[256,896]{1,0:T(8,128)}) custom-call(bf16[512,896]{1,0:T(8,128)(2,1)} %hidden.1, bf16[4096,896]{1,0:T(8,128)(2,1)} %weight.1, bf16[512,256]{1,0:T(8,128)(2,1)} %cotangent.1), custom_call_target="tpu_custom_call" | custom-call | tf_op jit(solution)/shard_map/pallas_call | solution.py:471
  97.1 1.7 %copy.9 = bf16[512,256]{1,0:T(8,128)(2,1)} copy(bf16[512,256]{1,0:T(8,128)(2,1)} %get-tuple-element.6) | data formatting | bytes 524288
  98.8 2.2 %copy.10 = bf16[512,896]{1,0:T(8,128)(2,1)} copy(bf16[512,896]{1,0:T(8,128)(2,1)} %get-tuple-element.7) | data formatting | bytes 1835008
  101.0 2.2 %copy.11 = f32[256,896]{1,0:T(8,128)} copy(f32[256,896]{1,0:T(8,128)} %get-tuple-element.8) | data formatting | bytes 1835008

commit v3 on v2

v3 whole, which is shorter than its diff:
```python
import functools

import jax
import jax.numpy as jnp
from jax import lax
from jax.experimental import pallas as pl
from jax.experimental.pallas import tpu as pltpu
from jax.sharding import PartitionSpec as P

MESH = pl.DeviceIdType.MESH
F32 = jnp.float32
BF16 = jnp.bfloat16
NX, NZ = 4, 8
HCH = 2
GROUPS = ((0, 512), (512, 384))
WCH = 4
ZR = 16


def zigzag(i, top):
    odd = lax.rem(i, 2)
    return top + (1 - odd) * (i // 2) - odd * ((i + 1) // 2)


def kernel(
    scale,
    hidden,
    weight,
    cotangent,
    output,
    hidden_grad,
    weight_grad,
    w,
    hid,
    hrel,
    cot,
    o_send,
    o_sum,
    xh,
    xf,
    yb,
    part,
    zs0,
    zs1,
    zb0,
    zb1,
    acc,
    load_sem,
    cy_s,
    cy_r,
    cx_s,
    cx_r,
    cd_s,
    cd_r,
    h_s,
    h_r,
    o_s,
    o_r,
    xo_s,
    xo_r,
    yo_s,
    yo_r,
    z_s,
    z_r,
):
    gx = lax.axis_index("gx")
    gy = lax.axis_index("gy")
    y_hi, z = gx // NZ, lax.rem(gx, NZ)
    c = lax.rem(gy, 2)
    x = lax.rem(gy // 2, NX)
    y_lo = gy // (2 * NX)
    tok, ff = hid.shape[1], hid.shape[2]
    feat = cot.shape[2]
    half = tok // 2
    rows = feat // 2

    def dev(yh, yl, xx, zz, cc):
        return (yh * NZ + zz, (yl * NX + xx) * 2 + cc)

    right, left = lax.rem(x + 1, NX), lax.rem(x + NX - 1, NX)
    across = lax.rem(x + 2, NX)
    core = dev(y_hi, y_lo, x, z, 1 - c)
    near = dev(y_hi, 1 - y_lo, x, z, c)
    far = dev(1 - y_hi, 1 - y_lo, x, z, c)
    first = dev(lax.rem(y_hi + c, 2), 1 - y_lo, x, z, c)
    second = dev(lax.rem(y_hi + 1 - c, 2), 1 - y_lo, x, z, c)
    x_dev = (dev(y_hi, y_lo, right, z, c), dev(y_hi, y_lo, left, z, c))
    z_dev = (
        dev(y_hi, y_lo, x, lax.rem(z + 1, NZ), c),
        dev(y_hi, y_lo, x, lax.rem(z + NZ - 1, NZ), c),
    )

    def rc(src, dst, ss, rs, to):
        return pltpu.make_async_remote_copy(
            src_ref=src, dst_ref=dst, send_sem=ss, recv_sem=rs, device_id=to, device_id_type=MESH
        )

    sent = []

    def go(make, *where):
        make(*where).start()
        sent.append((make, where))

    base = (y_hi * NX * 2, (1 - y_hi) * NX * 2, 16)
    middle = lax.rem(y_hi + y_lo, 2)

    def slot(kind, xx):
        return cot.at[base[kind] + xx * 2 + c]

    mine = cot.at[y_lo * NX * 2 + x * 2 + c]
    near_slot = cot.at[(1 - y_lo) * NX * 2 + x * 2 + c]
    far_slot = slot(2, x)
    ld_cot = pltpu.make_async_copy(cotangent, mine, load_sem.at[0])
    ld_hid = pltpu.make_async_copy(hidden, hid.at[0], load_sem.at[1])
    ld_cot.start()
    ld_hid.start()
    wrows = w.shape[0] // WCH
    ld_w = [
        pltpu.make_async_copy(
            weight.at[pl.ds(i * wrows, wrows)], w.at[pl.ds(i * wrows, wrows)], load_sem.at[2 + i]
        )
        for i in range(WCH)
    ]
    for copy in ld_w:
        copy.start()

    barrier = pltpu.get_barrier_semaphore()
    peers = (core, near, far, *x_dev, *z_dev)
    for peer in peers:
        pl.semaphore_signal(barrier, inc=1, device_id=peer, device_id_type=MESH)
    pl.semaphore_wait(barrier, len(peers))

    def half_of(ref, h):
        return ref.at[pl.ds(h * half, half)]

    def xs_full(kind, d, h):
        ref = half_of(slot(kind, x), h)
        return rc(ref, ref, cx_s.at[kind, d, h], cx_r.at[kind, d, h], x_dev[d])

    def xs_relay(kind, d):
        ref = half_of(slot(kind, (left, right)[d]), d)
        return rc(ref, ref, cx_s.at[kind, d, 2], cx_r.at[kind, d, 2], x_dev[d])

    def from_full(kind, d, h):
        ref = half_of(slot(kind, (left, right)[d]), h)
        return rc(ref, ref, cx_s.at[kind, d, h], cx_r.at[kind, d, h], x_dev[d])

    def from_relay(kind, d):
        ref = half_of(slot(kind, across), d)
        return rc(ref, ref, cx_s.at[kind, d, 2], cx_r.at[kind, d, 2], x_dev[d])

    def to_core(kind, j):
        ref = slot(kind, (x, left, right, across)[j])
        return rc(ref, ref, cd_s.at[kind, j], cd_r.at[kind, j], core)

    def from_core(kind, j):
        ref = cot.at[base[kind] + (x, left, right, across)[j] * 2 + 1 - c]
        return rc(ref, ref, cd_s.at[kind, j], cd_r.at[kind, j], core)

    def to_near(h):
        ref = half_of(mine, h)
        return rc(ref, ref, cy_s.at[0, h], cy_r.at[0, h], near)

    def from_near(h):
        ref = half_of(near_slot, h)
        return rc(ref, ref, cy_s.at[0, h], cy_r.at[0, h], near)

    def to_far(src, h):
        return rc(half_of(src, h), half_of(far_slot, h), cy_s.at[1, h], cy_r.at[1, h], far)

    def spread(kind, h):
        xs_full(kind, 0, h).start()
        xs_full(kind, 1, h).start()

    def relay(kind):
        for d in range(2):
            from_full(kind, d, d).wait_recv()
            xs_relay(kind, d).start()
        for d in range(2):
            from_full(kind, d, 1 - d).wait_recv()
            to_core(kind, 1 + d).start()

    def finish(kind):
        for d in range(2):
            from_relay(kind, d).wait_recv()
        to_core(kind, 3).start()

    outer, inner = pl.when(middle == 0), pl.when(middle == 1)

    ld_cot.wait()

    @outer
    def _():
        for h in range(2):
            to_near(h).start()
            spread(0, h)
        to_core(0, 0).start()

    @inner
    def _():
        for h in range(2):
            to_near(h).start()
            to_far(mine, h).start()
        spread(1, 0)
        to_core(1, 0).start()

    hrows = tok // HCH

    def hpiece(ref, g, i):
        return ref.at[pl.ds(i * hrows, hrows), pl.ds(*GROUPS[g])]

    def h_first(g, i):
        at = g, i
        return rc(hpiece(hid.at[0], g, i), hpiece(hrel, g, i), h_s.at[0, *at], h_r.at[0, *at], first)

    def h_second(g, i):
        at = g, i
        return rc(hpiece(hrel, g, i), hpiece(hid.at[1], g, i), h_s.at[1, *at], h_r.at[1, *at], second)

    def hrelay(g, i):
        h_first(g, i).wait_recv()
        go(h_second, g, i)

    ld_hid.wait()
    for i in range(HCH):
        go(h_first, 0, i)

    def out_part(t, cc):
        yp = lax.rem(y_lo + 1 + lax.rem(t, 2), 2)
        g = (yp * NX + lax.rem(x + zigzag(t // 2, 2), NX)) * 2 + cc
        wg = w[pl.ds(pl.multiple_of(g * feat, feat), feat), :]
        return lax.dot_general(hid[0], wg, (((1,), (1,)), ((), ())), preferred_element_type=F32)

    def o_copy(t):
        return rc(o_send.at[t], o_sum.at[t], o_s.at[t], o_r.at[t], core)

    def send_out(t, _):
        o_send[t] = out_part(t, 1 - c)
        o_copy(t).start()
        return 0

    def add_out(t, _):
        o_copy(t).wait_recv()
        o_sum[t] = o_sum[t] + out_part(t, c)
        return 0

    for copy in ld_w:
        copy.wait()
    lax.fori_loop(0, 6, send_out, 0)

    @outer
    def _():
        for h in range(2):
            from_near(h).wait_recv()
            to_far(near_slot, h).start()
        to_core(1, 0).start()
        relay(0)

    @inner
    def _():
        for h in range(2):
            from_near(h).wait_recv()
            spread(0, h)
            to_far(far_slot, h).wait_recv()
            spread(2, h)
        spread(1, 1)
        to_core(0, 0).start()
        to_core(2, 0).start()

    lax.fori_loop(6, 8, send_out, 0)
    hrelay(0, 0)

    @outer
    def _():
        for h in range(2):
            to_far(far_slot, h).wait_recv()
            spread(2, h)
        for h in range(2):
            spread(1, h)
        to_core(2, 0).start()

    hrelay(0, 1)
    for i in range(HCH):
        go(h_first, 1, i)
    lax.fori_loop(0, 2, add_out, 0)
    inner(lambda: relay(0))
    lax.fori_loop(2, 4, add_out, 0)
    relay(2)
    finish(0)
    hrelay(1, 0)
    lax.fori_loop(4, 6, add_out, 0)
    hrelay(1, 1)
    finish(2)
    relay(1)
    lax.fori_loop(6, 8, add_out, 0)

    def xo_half(d, q):
        src = o_sum.at[q].at[pl.ds(d * half, half)]
        return rc(src, xh.at[d, q], xo_s.at[0, d, q], xo_r.at[0, d, q], x_dev[d])

    def xo_full(d, q):
        return rc(o_sum.at[2 + 2 * d + q], xf.at[d, q], xo_s.at[1, d, q], xo_r.at[1, d, q], x_dev[d])

    for q in range(2):
        for d in range(2):
            go(xo_half, d, q)
    for kind in (0, 2):
        for j in range(4):
            from_core(kind, j).wait_recv()

    def w_part(g):
        def body(i, _):
            zz = lax.rem(z + zigzag(i, 4), NZ)
            dims = (((0,), (0,)), ((), ()))
            cols = pl.ds(*GROUPS[g])
            part[i, :, cols] = lax.dot_general(
                cot[y_hi * NZ + zz], hid[0, :, cols], dims, preferred_element_type=F32
            ) + lax.dot_general(cot[16 + zz], hid[1, :, cols], dims, preferred_element_type=F32)
            return 0

        return body

    index_of = {4: 0, 3: 1, 5: 2, 2: 3, 6: 4, 1: 5, 7: 6, 0: 7}

    zs, zb = (zs0, zs1), (zb0, zb1)
    quarter = rows // 4

    def z_rows(d, m):
        k = 4 - (m + 1) // 2
        return index_of[(k if d == 0 else -k) % NZ], ((m + d) % 2) * rows

    def z_copy(d, m, g):
        src = zs[g].at[d, m] if m < 2 else zb[g].at[d, m - 2]
        return rc(src, zb[g].at[d, m], z_s.at[g, d, m], z_r.at[g, d, m], z_dev[d])

    def coded(v):
        high = v.astype(BF16)
        near_v = high.astype(F32)
        fit = jnp.abs(near_v) > 1e-36
        ratio = jnp.where(fit, (v - near_v) / jnp.where(fit, near_v, 1.0), 0.0)
        return high, jnp.clip(jnp.round(ratio * 1792.0), -7.0, 7.0)

    def parted(p):
        q = jnp.round(p * (1.0 / 15.0))
        return q, p - 15.0 * q

    def take(ref, r):
        low = ref[pl.ds(rows + r, ZR)].astype(F32)
        size = jnp.abs(low)
        e = jnp.floor(jnp.log2(size) + 1.0 / 512.0)
        f = jnp.round((size * jnp.exp2(-e) - 1.0) * 128.0)
        codes = (*parted(e), *parted(jnp.where(low < 0.0, -f, f)))
        high = [ref[pl.ds(j * quarter + r, ZR)].astype(F32) for j in range(4)]
        return [h + h * (q * (1.0 / 1792.0)) for h, q in zip(high, codes)]

    def put(ref, r, values):
        q = []
        for j, v in enumerate(values):
            high, code = coded(v)
            ref[pl.ds(j * quarter + r, ZR)] = high
            q.append(code)
        e, f = q[0] * 15.0 + q[1], q[2] * 15.0 + q[3]
        size = jnp.exp2(e) * (1.0 + jnp.abs(f) * (1.0 / 128.0))
        ref[pl.ds(rows + r, ZR)] = jnp.where(f < 0.0, -size, size).astype(BF16)

    def in_rows(run):
        def body(i, _):
            run(pl.multiple_of(i * ZR, ZR))
            return 0

        lax.fori_loop(0, quarter // ZR, body, 0)

    def part_rows(i, start, r, g):
        return [part[i, pl.ds(start + j * quarter + r, ZR), pl.ds(*GROUPS[g])] for j in range(4)]

    def z_first(d, m, g):
        i, start = z_rows(d, m)
        in_rows(lambda r: put(zs[g].at[d, m], r, part_rows(i, start, r, g)))
        go(z_copy, d, m, g)

    def z_one(d, m, g):
        z_copy(d, m - 2, g).wait_recv()
        i, start = z_rows(d, m)
        ref = zb[g].at[d, m - 2]

        def run(r):
            own = part_rows(i, start, r, g)
            put(ref, r, [s + p for s, p in zip(take(ref, r), own)])

        in_rows(run)
        go(z_copy, d, m, g)

    def z_step(m):
        for g in range(2):
            z_one(0, m, g)
            z_one(1, m, g)

    def z_start(g):
        for i in range(HCH):
            h_second(g, i).wait_recv()
        run = w_part(g)
        lax.fori_loop(0, 1, run, 0)
        z_first(0, 0, g)
        z_first(1, 0, g)
        lax.fori_loop(1, 3, run, 0)
        z_first(0, 1, g)
        z_first(1, 1, g)

    z_start(0)
    z_start(1)
    lax.fori_loop(3, 8, w_part(0), 0)
    lax.fori_loop(3, 8, w_part(1), 0)
    finish(1)
    for j in range(4):
        from_core(1, j).wait_recv()

    def h_part(g, _):
        acc[...] = acc[...] + jnp.dot(
            cot[g], w[pl.ds(pl.multiple_of(g * feat, feat), feat), :], preferred_element_type=F32
        )
        return 0

    def xo_add(q):
        xo_half(0, q).wait_recv()
        o_sum[2 + q, pl.ds(0, half)] = o_sum[2 + q, pl.ds(0, half)] + xh[0, q]
        go(xo_full, 0, q)
        xo_half(1, q).wait_recv()
        o_sum[4 + q, pl.ds(half, half)] = o_sum[4 + q, pl.ds(half, half)] + xh[1, q]
        go(xo_full, 1, q)

    def xo_end(q):
        for d in range(2):
            xo_full(d, q).wait_recv()
        o_sum[6 + q] = o_sum[6 + q] + xf[0, q] + xf[1, q]

    def yo():
        return rc(o_sum.at[6], yb, yo_s.at[0], yo_r.at[0], near)

    xo_add(0)
    xo_add(1)
    acc[...] = jnp.dot(cot[0], w[pl.ds(0, feat), :], preferred_element_type=F32)
    lax.fori_loop(1, 8, h_part, 0)
    z_step(2)
    lax.fori_loop(8, 16, h_part, 0)
    hidden_grad[...] = acc[...].astype(BF16)
    z_step(3)
    z_step(4)
    xo_end(0)
    go(yo)
    z_step(5)
    xo_end(1)
    z_step(6)
    yo().wait_recv()
    output[...] = (o_sum[7] + yb[...]).astype(BF16)

    def z_end(start, m0, m1, g):
        z_copy(0, m0, g).wait_recv()
        z_copy(1, m1, g).wait_recv()

        def run(r):
            own = part_rows(7, start, r, g)
            sums = zip(own, take(zb[g].at[0, m0], r), take(zb[g].at[1, m1], r))
            for j, (p, s, t) in enumerate(sums):
                weight_grad[pl.ds(start + j * quarter + r, ZR), pl.ds(*GROUPS[g])] = (p + s + t) * scale

        in_rows(run)

    for h in range(2):
        to_near(h).wait_send()
        to_far(mine, h).wait_send()
    for kind in range(3):
        for d in range(2):
            for h in range(2):
                xs_full(kind, d, h).wait_send()
            xs_relay(kind, d).wait_send()
        for j in range(4):
            to_core(kind, j).wait_send()

    def sent_out(t, _):
        o_copy(t).wait_send()
        return 0

    lax.fori_loop(0, 8, sent_out, 0)
    for g in range(2):
        z_end(0, 6, 5, g)
        z_end(rows, 5, 6, g)
    for make, where in sent:
        make(*where).wait_send()


def store(a, b, d, a_out, b_out, d_out, sems):
    pairs = ((a, a_out), (b, b_out), (d, d_out))
    copies = [pltpu.make_async_copy(s, t, sems.at[i]) for i, (s, t) in enumerate(pairs)]
    for copy in copies:
        copy.start()
    for copy in copies:
        copy.wait()


def shards(hidden, weight, cotangent):
    tok, ff = hidden.shape
    d_all = weight.shape[0]
    feat = cotangent.shape[1]
    scale = float(tok * lax.axis_size("gx")) ** (-0.5)
    any_space = pl.BlockSpec(memory_space=pl.ANY)
    vmem_space = pl.BlockSpec(memory_space=pltpu.VMEM)
    sem = pltpu.SemaphoreType.DMA
    v = pltpu.VMEM
    shapes = (((tok, feat), BF16), ((tok, ff), BF16), ((feat, ff), F32))
    args = [pltpu.with_memory_space_constraint(a, pltpu.HBM) for a in (hidden, weight, cotangent)]
    results = pl.pallas_call(
        functools.partial(kernel, scale),
        out_shape=tuple(v(*shape) for shape in shapes),
        in_specs=[any_space] * 3,
        out_specs=(vmem_space,) * 3,
        scratch_shapes=[
            v((d_all, ff), BF16),
            v((2, tok, ff), BF16),
            v((tok, ff), BF16),
            v((24, tok, feat), BF16),
            v((8, tok, feat), F32),
            v((8, tok, feat), F32),
            v((2, 2, tok // 2, feat), F32),
            v((2, 2, tok, feat), F32),
            v((tok, feat), F32),
            v((8, feat, ff), F32),
            *(v((2, n, feat * 5 // 8, size), BF16) for n in (2, 7) for _, size in GROUPS),
            v((tok, ff), F32),
            sem((2 + WCH,)),
            sem((2, 2)),
            sem((2, 2)),
            sem((3, 2, 3)),
            sem((3, 2, 3)),
            sem((3, 4)),
            sem((3, 4)),
            sem((2, 2, HCH)),
            sem((2, 2, HCH)),
            sem((8,)),
            sem((8,)),
            sem((2, 2, 2)),
            sem((2, 2, 2)),
            sem((1,)),
            sem((1,)),
            sem((2, 2, 7)),
            sem((2, 2, 7)),
        ],
        compiler_params=pltpu.CompilerParams(
            collective_id=0, has_side_effects=True, vmem_limit_bytes=50 * 1024 * 1024
        ),
    )(*args)
    return pl.pallas_call(
        store,
        out_shape=tuple(jax.ShapeDtypeStruct(*shape) for shape in shapes),
        in_specs=[any_space] * 3,
        out_specs=(pl.BlockSpec(memory_space=pltpu.HBM),) * 3,
        scratch_shapes=[sem((3,))],
        compiler_params=pltpu.CompilerParams(vmem_limit_bytes=1024 * 1024),
    )(*results)


def solution(mesh):
    placed = (P("gx", "gy"), P(None, "gy"), P("gx", "gy"))
    return jax.shard_map(
        shards,
        mesh=mesh,
        in_specs=placed,
        out_specs=(P("gx", "gy"), P("gx", "gy"), P("gx", "gy")),
        check_vma=False,
    )
```

time: 103 us -> 90.5 us (0.88)
  Pallas kernels: 96.5 us -> 89.8 us
  local copies, waits for them, and re-layouts: 6 us -> 0 us
    pallas_call x1 -> x2, Pallas kernels: 96.5 us -> 89.8 us  [the longest x1 88.5 us: shards(): pl.pallas_call(functools.partial(kernel, scale), out_shape=tuple((v(*shap...]
    unnamed x3 -> x0, local copies, waits for them, and re-layouts: 6 us -> none
where the time goes in v3:
time: 90.5 us; the launch traced here: 90.4 us
  Pallas kernels  89.8 us (99%)
    pallas_call x1, Pallas kernels, shards(): pl.pallas_call(functools.partial(kernel, scale), out_shape=tuple((v(*shap...  88.5 us

profile of v3, /device:TPU:1, one launch (start us, length us, event | category | flops | bytes accessed | tf_op | source)
XLA Modules:
  0.0 90.4 jit_solution(6232985961413189203)
XLA Ops:
  0.6 88.5 %shard_map.58 = (bf16[512,256]{1,0:T(8,128)(2,1)S(1)}, bf16[512,896]{1,0:T(8,128)(2,1)S(1)}, f32[256,896]{1,0:T(8,128)S(1)}) custom-call(bf16[512,896]{1,0:T(8,128)(2,1)} %hidden.1, bf16[4096,896]{1,0:T(8,128)(2,1)} %weight.1, bf16[512,256]{1,0:T(8,128)(2,1)} %cotangent.1), custom_call_target="tpu_custom_call" | custom-call | tf_op jit(solution)/shard_map/pallas_call | solution.py:511
  89.1 1.3 %shard_map.59 = (bf16[512,256]{1,0:T(8,128)(2,1)}, bf16[512,896]{1,0:T(8,128)(2,1)}, f32[256,896]{1,0:T(8,128)}) custom-call(bf16[512,256]{1,0:T(8,128)(2,1)S(1)} %get-tuple-element.6.a, bf16[512,896]{1,0:T(8,128)(2,1)S(1)} %get-tuple-element.7.b, f32[256,896]{1,0:T(8,128)S(1)} %get-tuple-element.8.d), custom_call_target="tpu_custom_call" | custom-call | tf_op jit(solution)/shard_map/pallas_call | solution.py:551

commit v4 on v3

--- a/solution.py
+++ b/solution.py
@@ -45,7 +45,10 @@
     zb0,
     zb1,
     acc,
+    hgb,
+    outb,
     load_sem,
+    store_sem,
     cy_s,
     cy_r,
     cx_s,
@@ -263,7 +266,6 @@
             spread(0, h)
             to_far(far_slot, h).wait_recv()
             spread(2, h)
-        spread(1, 1)
         to_core(0, 0).start()
         to_core(2, 0).start()
 
@@ -272,27 +274,34 @@
 
     @outer
     def _():
-        for h in range(2):
-            to_far(far_slot, h).wait_recv()
-            spread(2, h)
-        for h in range(2):
-            spread(1, h)
+        to_far(far_slot, 0).wait_recv()
+        spread(2, 0)
+        hrelay(0, 1)
+        to_far(far_slot, 1).wait_recv()
+        spread(2, 1)
+        for i in range(HCH):
+            h_first(1, i).start()
         to_core(2, 0).start()
 
-    hrelay(0, 1)
-    for i in range(HCH):
-        go(h_first, 1, i)
+    @inner
+    def _():
+        h_first(0, 1).wait_recv()
+        h_second(0, 1).start()
+        for i in range(HCH):
+            h_first(1, i).start()
+
+    sent.extend((h_first, (1, i)) for i in range(HCH))
     lax.fori_loop(0, 2, add_out, 0)
     inner(lambda: relay(0))
     lax.fori_loop(2, 4, add_out, 0)
     relay(2)
+    outer(lambda: spread(1, 0))
+    spread(1, 1)
     finish(0)
     hrelay(1, 0)
     lax.fori_loop(4, 6, add_out, 0)
+    finish(2)
     hrelay(1, 1)
-    finish(2)
-    relay(1)
-    lax.fori_loop(6, 8, add_out, 0)
 
     def xo_half(d, q):
         src = o_sum.at[q].at[pl.ds(d * half, half)]
@@ -301,9 +310,14 @@
     def xo_full(d, q):
         return rc(o_sum.at[2 + 2 * d + q], xf.at[d, q], xo_s.at[1, d, q], xo_r.at[1, d, q], x_dev[d])
 
-    for q in range(2):
-        for d in range(2):
-            go(xo_half, d, q)
+    def xo_add(q):
+        xo_half(0, q).wait_recv()
+        o_sum[2 + q, pl.ds(0, half)] = o_sum[2 + q, pl.ds(0, half)] + xh[0, q]
+        go(xo_full, 0, q)
+        xo_half(1, q).wait_recv()
+        o_sum[4 + q, pl.ds(half, half)] = o_sum[4 + q, pl.ds(half, half)] + xh[1, q]
+        go(xo_full, 1, q)
+
     for kind in (0, 2):
         for j in range(4):
             from_core(kind, j).wait_recv()
@@ -406,13 +420,9 @@
         z_first(0, 1, g)
         z_first(1, 1, g)
 
-    z_start(0)
-    z_start(1)
-    lax.fori_loop(3, 8, w_part(0), 0)
-    lax.fori_loop(3, 8, w_part(1), 0)
-    finish(1)
-    for j in range(4):
-        from_core(1, j).wait_recv()
+    def z_pair(m, g):
+        z_one(0, m, g)
+        z_one(1, m, g)
 
     def h_part(g, _):
         acc[...] = acc[...] + jnp.dot(
@@ -420,14 +430,6 @@
         )
         return 0
 
-    def xo_add(q):
-        xo_half(0, q).wait_recv()
-        o_sum[2 + q, pl.ds(0, half)] = o_sum[2 + q, pl.ds(0, half)] + xh[0, q]
-        go(xo_full, 0, q)
-        xo_half(1, q).wait_recv()
-        o_sum[4 + q, pl.ds(half, half)] = o_sum[4 + q, pl.ds(half, half)] + xh[1, q]
-        go(xo_full, 1, q)
-
     def xo_end(q):
         for d in range(2):
             xo_full(d, q).wait_recv()
@@ -436,22 +438,41 @@
     def yo():
         return rc(o_sum.at[6], yb, yo_s.at[0], yo_r.at[0], near)
 
+    z_start(0)
+    relay(1)
+    for q in range(2):
+        for d in range(2):
+            go(xo_half, d, q)
+    z_start(1)
+    lax.fori_loop(6, 8, add_out, 0)
+    z_pair(2, 0)
+    lax.fori_loop(3, 8, w_part(0), 0)
+    z_pair(3, 0)
     xo_add(0)
+    z_pair(2, 1)
+    lax.fori_loop(3, 8, w_part(1), 0)
+    z_pair(3, 1)
+    finish(1)
     xo_add(1)
+    for j in range(4):
+        from_core(1, j).wait_recv()
+    z_pair(4, 0)
     acc[...] = jnp.dot(cot[0], w[pl.ds(0, feat), :], preferred_element_type=F32)
-    lax.fori_loop(1, 8, h_part, 0)
-    z_step(2)
-    lax.fori_loop(8, 16, h_part, 0)
-    hidden_grad[...] = acc[...].astype(BF16)
-    z_step(3)
-    z_step(4)
+    lax.fori_loop(1, 4, h_part, 0)
+    z_pair(4, 1)
+    lax.fori_loop(4, 9, h_part, 0)
+    z_pair(5, 0)
+    lax.fori_loop(9, 13, h_part, 0)
+    z_pair(5, 1)
     xo_end(0)
     go(yo)
-    z_step(5)
+    lax.fori_loop(13, 16, h_part, 0)
+    hgb[...] = acc[...].astype(BF16)
+    st_hg = pltpu.make_async_copy(hgb, hidden_grad, store_sem.at[0])
+    st_hg.start()
+    z_pair(6, 0)
+    z_pair(6, 1)
     xo_end(1)
-    z_step(6)
-    yo().wait_recv()
-    output[...] = (o_sum[7] + yb[...]).astype(BF16)
 
     def z_end(start, m0, m1, g):
         z_copy(0, m0, g).wait_recv()
@@ -461,9 +482,13 @@
             own = part_rows(7, start, r, g)
             sums = zip(own, take(zb[g].at[0, m0], r), take(zb[g].at[1, m1], r))
             for j, (p, s, t) in enumerate(sums):
-                weight_grad[pl.ds(start + j * quarter + r, ZR), pl.ds(*GROUPS[g])] = (p + s + t) * scale
+                part[7, pl.ds(start + j * quarter + r, ZR), pl.ds(*GROUPS[g])] = (p + s + t) * scale
 
         in_rows(run)
+
+    def st_wg(g):
+        cols = pl.ds(*GROUPS[g])
+        return pltpu.make_async_copy(part.at[7, :, cols], weight_grad.at[:, cols], store_sem.at[2 + g])
 
     for h in range(2):
         to_near(h).wait_send()
@@ -481,11 +506,22 @@
         return 0
 
     lax.fori_loop(0, 8, sent_out, 0)
-    for g in range(2):
-        z_end(0, 6, 5, g)
-        z_end(rows, 5, 6, g)
+    z_end(0, 6, 5, 0)
+    z_end(rows, 5, 6, 0)
+    st_wg(0).start()
+    yo().wait_recv()
+    outb[...] = (o_sum[7] + yb[...]).astype(BF16)
+    st_out = pltpu.make_async_copy(outb, output, store_sem.at[1])
+    st_out.start()
+    z_end(0, 6, 5, 1)
+    z_end(rows, 5, 6, 1)
+    st_wg(1).start()
     for make, where in sent:
         make(*where).wait_send()
+    st_hg.wait()
+    st_out.wait()
+    for g in range(2):
+        st_wg(g).wait()
 
 
 def store(a, b, d, a_out, b_out, d_out, sems):
@@ -503,7 +539,6 @@
     feat = cotangent.shape[1]
     scale = float(tok * lax.axis_size("gx")) ** (-0.5)
     any_space = pl.BlockSpec(memory_space=pl.ANY)
-    vmem_space = pl.BlockSpec(memory_space=pltpu.VMEM)
     sem = pltpu.SemaphoreType.DMA
     v = pltpu.VMEM
     shapes = (((tok, feat), BF16), ((tok, ff), BF16), ((feat, ff), F32))
@@ -512,7 +547,7 @@
         functools.partial(kernel, scale),
         out_shape=tuple(v(*shape) for shape in shapes),
         in_specs=[any_space] * 3,
-        out_specs=(vmem_space,) * 3,
+        out_specs=(any_space,) * 3,
         scratch_shapes=[
             v((d_all, ff), BF16),
             v((2, tok, ff), BF16),
@@ -526,7 +561,10 @@
             v((8, feat, ff), F32),
             *(v((2, n, feat * 5 // 8, size), BF16) for n in (2, 7) for _, size in GROUPS),
             v((tok, ff), F32),
+            v((tok, ff), BF16),
+            v((tok, feat), BF16),
             sem((2 + WCH,)),
+            sem((4,)),
             sem((2, 2)),
             sem((2, 2)),
             sem((3, 2, 3)),

time: 90.5 us -> 83.5 us (0.923)
  Pallas kernels: 89.8 us -> 82.7 us
    pallas_call x1, Pallas kernels: 88.5 us -> 81.4 us  [shards(): pl.pallas_call(functools.partial(kernel, scale), out_shape=tuple((v(*shap...]
where the time goes in v4:
time: 83.5 us; the launch traced here: 83.4 us
  Pallas kernels  82.7 us (99%)
    pallas_call x1, Pallas kernels, shards(): pl.pallas_call(functools.partial(kernel, scale), out_shape=tuple((v(*shap...  81.4 us

profile of v4, /device:TPU:1, one launch (start us, length us, event | category | flops | bytes accessed | tf_op | source)
XLA Modules:
  0.0 83.4 jit_solution(5663891895912756658)
XLA Ops:
  0.6 81.4 %shard_map.58 = (bf16[512,256]{1,0:T(8,128)(2,1)S(1)}, bf16[512,896]{1,0:T(8,128)(2,1)S(1)}, f32[256,896]{1,0:T(8,128)S(1)}) custom-call(bf16[512,896]{1,0:T(8,128)(2,1)} %hidden.1, bf16[4096,896]{1,0:T(8,128)(2,1)} %weight.1, bf16[512,256]{1,0:T(8,128)(2,1)} %cotangent.1), custom_call_target="tpu_custom_call" | custom-call | tf_op jit(solution)/shard_map/pallas_call | solution.py:546
  82.0 1.3 %shard_map.59 = (bf16[512,256]{1,0:T(8,128)(2,1)}, bf16[512,896]{1,0:T(8,128)(2,1)}, f32[256,896]{1,0:T(8,128)}) custom-call(bf16[512,256]{1,0:T(8,128)(2,1)S(1)} %get-tuple-element.6.a, bf16[512,896]{1,0:T(8,128)(2,1)S(1)} %get-tuple-element.7.b, f32[256,896]{1,0:T(8,128)S(1)} %get-tuple-element.8.d), custom_call_target="tpu_custom_call" | custom-call | tf_op jit(solution)/shard_map/pallas_call | solution.py:589

commit v5 on v4

--- a/solution.py
+++ b/solution.py
@@ -14,7 +14,8 @@
 HCH = 2
 GROUPS = ((0, 512), (512, 384))
 WCH = 4
-ZR = 16
+ZR = 32
+BOOST = 2.0**40
 
 
 def zigzag(i, top):
@@ -292,31 +293,45 @@
 
     sent.extend((h_first, (1, i)) for i in range(HCH))
     lax.fori_loop(0, 2, add_out, 0)
+    def xo_half(d, q):
+        src = half_of(o_sum.at[q], d)
+        return rc(src, xh.at[d, q], xo_s.at[d, q, 2], xo_r.at[d, q, 2], x_dev[d])
+
+    def xo_full(d, q, h):
+        src = half_of(o_sum.at[2 + 2 * d + q], h)
+        return rc(src, half_of(xf.at[d, q], h), xo_s.at[d, q, h], xo_r.at[d, q, h], x_dev[d])
+
+    def xo_add(q):
+        for d in range(2):
+            go(xo_full, d, q, 1 - d)
+        for d in range(2):
+            xo_half(d, q).wait_recv()
+            at = 2 + 2 * d + q, pl.ds(d * half, half)
+            o_sum[at] = o_sum[at] + xh[d, q]
+            go(xo_full, d, q, d)
+
+    def xo_end(q, h):
+        at = pl.ds(h * half, half)
+        for d in range(2):
+            xo_full(d, q, h).wait_recv()
+        o_sum[6 + q, at] = o_sum[6 + q, at] + xf[0, q, at] + xf[1, q, at]
+
+    def yo(h):
+        return rc(half_of(o_sum.at[6], h), half_of(yb, h), yo_s.at[h], yo_r.at[h], near)
+
     inner(lambda: relay(0))
     lax.fori_loop(2, 4, add_out, 0)
     relay(2)
     outer(lambda: spread(1, 0))
     spread(1, 1)
+    for q in range(2):
+        for d in range(2):
+            go(xo_half, d, q)
     finish(0)
     hrelay(1, 0)
     lax.fori_loop(4, 6, add_out, 0)
     finish(2)
     hrelay(1, 1)
-
-    def xo_half(d, q):
-        src = o_sum.at[q].at[pl.ds(d * half, half)]
-        return rc(src, xh.at[d, q], xo_s.at[0, d, q], xo_r.at[0, d, q], x_dev[d])
-
-    def xo_full(d, q):
-        return rc(o_sum.at[2 + 2 * d + q], xf.at[d, q], xo_s.at[1, d, q], xo_r.at[1, d, q], x_dev[d])
-
-    def xo_add(q):
-        xo_half(0, q).wait_recv()
-        o_sum[2 + q, pl.ds(0, half)] = o_sum[2 + q, pl.ds(0, half)] + xh[0, q]
-        go(xo_full, 0, q)
-        xo_half(1, q).wait_recv()
-        o_sum[4 + q, pl.ds(half, half)] = o_sum[4 + q, pl.ds(half, half)] + xh[1, q]
-        go(xo_full, 1, q)
 
     for kind in (0, 2):
         for j in range(4):
@@ -337,7 +352,6 @@
     index_of = {4: 0, 3: 1, 5: 2, 2: 3, 6: 4, 1: 5, 7: 6, 0: 7}
 
     zs, zb = (zs0, zs1), (zb0, zb1)
-    quarter = rows // 4
 
     def z_rows(d, m):
         k = 4 - (m + 1) // 2
@@ -347,67 +361,66 @@
         src = zs[g].at[d, m] if m < 2 else zb[g].at[d, m - 2]
         return rc(src, zb[g].at[d, m], z_s.at[g, d, m], z_r.at[g, d, m], z_dev[d])
 
-    def coded(v):
-        high = v.astype(BF16)
-        near_v = high.astype(F32)
-        fit = jnp.abs(near_v) > 1e-36
-        ratio = jnp.where(fit, (v - near_v) / jnp.where(fit, near_v, 1.0), 0.0)
-        return high, jnp.clip(jnp.round(ratio * 1792.0), -7.0, 7.0)
-
-    def parted(p):
-        q = jnp.round(p * (1.0 / 15.0))
-        return q, p - 15.0 * q
-
-    def take(ref, r):
-        low = ref[pl.ds(rows + r, ZR)].astype(F32)
-        size = jnp.abs(low)
-        e = jnp.floor(jnp.log2(size) + 1.0 / 512.0)
-        f = jnp.round((size * jnp.exp2(-e) - 1.0) * 128.0)
-        codes = (*parted(e), *parted(jnp.where(low < 0.0, -f, f)))
-        high = [ref[pl.ds(j * quarter + r, ZR)].astype(F32) for j in range(4)]
-        return [h + h * (q * (1.0 / 1792.0)) for h, q in zip(high, codes)]
-
-    def put(ref, r, values):
-        q = []
-        for j, v in enumerate(values):
-            high, code = coded(v)
-            ref[pl.ds(j * quarter + r, ZR)] = high
-            q.append(code)
-        e, f = q[0] * 15.0 + q[1], q[2] * 15.0 + q[3]
-        size = jnp.exp2(e) * (1.0 + jnp.abs(f) * (1.0 / 128.0))
-        ref[pl.ds(rows + r, ZR)] = jnp.where(f < 0.0, -size, size).astype(BF16)
+    def bound_in(ref):
+        return ref[pl.ds(rows, 8)].astype(F32)[0:1]
+
+    def take(ref, r, unit):
+        word = ref[pl.ds(r, ZR)].astype(F32)
+        size = jnp.exp2(jnp.log2(jnp.maximum(jnp.abs(word), 1e-37)) * 0.125) * unit
+        return jnp.where(word < 0.0, -size, size)
+
+    def put(ref, load, bound):
+        top = (bound * 1.0078125).astype(BF16)
+        ref[pl.ds(rows, 8)] = jnp.broadcast_to(top, (8, top.shape[1]))
+        top = top.astype(F32)
+        fit = top > 1e-33
+        inverse = jnp.where(fit, 32768.0 / jnp.where(fit, top, 1.0), 0.0)
+
+        def run(r):
+            v = load(r)
+            u = v * inverse
+            u2 = u * u
+            u4 = u2 * u2
+            u8 = u4 * u4
+            ref[pl.ds(r, ZR)] = jnp.where(v < 0.0, -u8, u8).astype(BF16)
+
+        in_rows(run)
 
     def in_rows(run):
         def body(i, _):
             run(pl.multiple_of(i * ZR, ZR))
             return 0
 
-        lax.fori_loop(0, quarter // ZR, body, 0)
+        lax.fori_loop(0, rows // ZR, body, 0)
 
     def part_rows(i, start, r, g):
-        return [part[i, pl.ds(start + j * quarter + r, ZR), pl.ds(*GROUPS[g])] for j in range(4)]
+        return part[i, pl.ds(start + r, ZR), pl.ds(*GROUPS[g])] * BOOST
+
+    def peak_of(i, start, g):
+        def body(n, peak):
+            return jnp.maximum(peak, jnp.abs(part_rows(i, start, pl.multiple_of(n * ZR, ZR), g)))
+
+        peak = lax.fori_loop(0, rows // ZR, body, jnp.zeros((ZR, GROUPS[g][1]), F32))
+        return jnp.max(peak, axis=0, keepdims=True)
 
     def z_first(d, m, g):
         i, start = z_rows(d, m)
-        in_rows(lambda r: put(zs[g].at[d, m], r, part_rows(i, start, r, g)))
+        put(zs[g].at[d, m], lambda r: part_rows(i, start, r, g), peak_of(i, start, g))
         go(z_copy, d, m, g)
 
     def z_one(d, m, g):
+        i, start = z_rows(d, m)
+        peak = peak_of(i, start, g)
         z_copy(d, m - 2, g).wait_recv()
-        i, start = z_rows(d, m)
         ref = zb[g].at[d, m - 2]
-
-        def run(r):
-            own = part_rows(i, start, r, g)
-            put(ref, r, [s + p for s, p in zip(take(ref, r), own)])
-
-        in_rows(run)
+        bound = bound_in(ref)
+        unit = bound * (1.0 / 32768.0)
+        put(ref, lambda r: take(ref, r, unit) + part_rows(i, start, r, g), bound + peak)
         go(z_copy, d, m, g)
 
-    def z_step(m):
-        for g in range(2):
-            z_one(0, m, g)
-            z_one(1, m, g)
+    def z_pair(m, g):
+        z_one(0, m, g)
+        z_one(1, m, g)
 
     def z_start(g):
         for i in range(HCH):
@@ -420,29 +433,14 @@
         z_first(0, 1, g)
         z_first(1, 1, g)
 
-    def z_pair(m, g):
-        z_one(0, m, g)
-        z_one(1, m, g)
-
     def h_part(g, _):
         acc[...] = acc[...] + jnp.dot(
             cot[g], w[pl.ds(pl.multiple_of(g * feat, feat), feat), :], preferred_element_type=F32
         )
         return 0
 
-    def xo_end(q):
-        for d in range(2):
-            xo_full(d, q).wait_recv()
-        o_sum[6 + q] = o_sum[6 + q] + xf[0, q] + xf[1, q]
-
-    def yo():
-        return rc(o_sum.at[6], yb, yo_s.at[0], yo_r.at[0], near)
-
     z_start(0)
     relay(1)
-    for q in range(2):
-        for d in range(2):
-            go(xo_half, d, q)
     z_start(1)
     lax.fori_loop(6, 8, add_out, 0)
     z_pair(2, 0)
@@ -460,35 +458,39 @@
     acc[...] = jnp.dot(cot[0], w[pl.ds(0, feat), :], preferred_element_type=F32)
     lax.fori_loop(1, 4, h_part, 0)
     z_pair(4, 1)
+    xo_end(0, 0)
+    go(yo, 0)
     lax.fori_loop(4, 9, h_part, 0)
     z_pair(5, 0)
     lax.fori_loop(9, 13, h_part, 0)
     z_pair(5, 1)
-    xo_end(0)
-    go(yo)
+    xo_end(0, 1)
+    go(yo, 1)
     lax.fori_loop(13, 16, h_part, 0)
     hgb[...] = acc[...].astype(BF16)
     st_hg = pltpu.make_async_copy(hgb, hidden_grad, store_sem.at[0])
     st_hg.start()
     z_pair(6, 0)
     z_pair(6, 1)
-    xo_end(1)
+    xo_end(1, 0)
+    xo_end(1, 1)
 
     def z_end(start, m0, m1, g):
         z_copy(0, m0, g).wait_recv()
         z_copy(1, m1, g).wait_recv()
 
+        refs = zb[g].at[0, m0], zb[g].at[1, m1]
+        unit0, unit1 = (bound_in(ref) * (1.0 / 32768.0) for ref in refs)
+
         def run(r):
-            own = part_rows(7, start, r, g)
-            sums = zip(own, take(zb[g].at[0, m0], r), take(zb[g].at[1, m1], r))
-            for j, (p, s, t) in enumerate(sums):
-                part[7, pl.ds(start + j * quarter + r, ZR), pl.ds(*GROUPS[g])] = (p + s + t) * scale
+            v = part_rows(7, start, r, g) + take(refs[0], r, unit0) + take(refs[1], r, unit1)
+            part[7, pl.ds(start + r, ZR), pl.ds(*GROUPS[g])] = v * (scale / BOOST)
 
         in_rows(run)
 
-    def st_wg(g):
-        cols = pl.ds(*GROUPS[g])
-        return pltpu.make_async_copy(part.at[7, :, cols], weight_grad.at[:, cols], store_sem.at[2 + g])
+    def st_wg(g, i):
+        at = pl.ds(i * rows, rows), pl.ds(*GROUPS[g])
+        return pltpu.make_async_copy(part.at[7, *at], weight_grad.at[*at], store_sem.at[2 + 2 * g + i])
 
     for h in range(2):
         to_near(h).wait_send()
@@ -507,21 +509,25 @@
 
     lax.fori_loop(0, 8, sent_out, 0)
     z_end(0, 6, 5, 0)
+    st_wg(0, 0).start()
     z_end(rows, 5, 6, 0)
-    st_wg(0).start()
-    yo().wait_recv()
+    st_wg(0, 1).start()
+    for h in range(2):
+        yo(h).wait_recv()
     outb[...] = (o_sum[7] + yb[...]).astype(BF16)
     st_out = pltpu.make_async_copy(outb, output, store_sem.at[1])
     st_out.start()
     z_end(0, 6, 5, 1)
+    st_wg(1, 0).start()
     z_end(rows, 5, 6, 1)
-    st_wg(1).start()
+    st_wg(1, 1).start()
     for make, where in sent:
         make(*where).wait_send()
     st_hg.wait()
     st_out.wait()
     for g in range(2):
-        st_wg(g).wait()
+        for i in range(2):
+            st_wg(g, i).wait()
 
 
 def store(a, b, d, a_out, b_out, d_out, sems):
@@ -559,12 +565,12 @@
             v((2, 2, tok, feat), F32),
             v((tok, feat), F32),
             v((8, feat, ff), F32),
-            *(v((2, n, feat * 5 // 8, size), BF16) for n in (2, 7) for _, size in GROUPS),
+            *(v((2, n, feat // 2 + 8, size), BF16) for n in (2, 7) for _, size in GROUPS),
             v((tok, ff), F32),
             v((tok, ff), BF16),
             v((tok, feat), BF16),
             sem((2 + WCH,)),
-            sem((4,)),
+            sem((6,)),
             sem((2, 2)),
             sem((2, 2)),
             sem((3, 2, 3)),
@@ -575,10 +581,10 @@
             sem((2, 2, HCH)),
             sem((8,)),
             sem((8,)),
-            sem((2, 2, 2)),
-            sem((2, 2, 2)),
-            sem((1,)),
-            sem((1,)),
+            sem((2, 2, 3)),
+            sem((2, 2, 3)),
+            sem((2,)),
+            sem((2,)),
             sem((2, 2, 7)),
             sem((2, 2, 7)),
         ],

time: 83.5 us -> 80 us (0.958)
  Pallas kernels: 82.7 us -> 79.3 us
    pallas_call x1, Pallas kernels: 81.4 us -> 77.9 us  [shards(): pl.pallas_call(functools.partial(kernel, scale), out_shape=tuple((v(*shap...]
where the time goes in v5:
time: 80 us; the launch traced here: 79.9 us
  Pallas kernels  79.3 us (99%)
    pallas_call x1, Pallas kernels, shards(): pl.pallas_call(functools.partial(kernel, scale), out_shape=tuple((v(*shap...  77.9 us

profile of v5, /device:TPU:1, one launch (start us, length us, event | category | flops | bytes accessed | tf_op | source)
XLA Modules:
  0.0 79.9 jit_solution(16066961949989768196)
XLA Ops:
  0.6 77.9 %shard_map.58 = (bf16[512,256]{1,0:T(8,128)(2,1)S(1)}, bf16[512,896]{1,0:T(8,128)(2,1)S(1)}, f32[256,896]{1,0:T(8,128)S(1)}) custom-call(bf16[512,896]{1,0:T(8,128)(2,1)} %hidden.1, bf16[4096,896]{1,0:T(8,128)(2,1)} %weight.1, bf16[512,256]{1,0:T(8,128)(2,1)} %cotangent.1), custom_call_target="tpu_custom_call" | custom-call | tf_op jit(solution)/shard_map/pallas_call | solution.py:552
  78.6 1.3 %shard_map.59 = (bf16[512,256]{1,0:T(8,128)(2,1)}, bf16[512,896]{1,0:T(8,128)(2,1)}, f32[256,896]{1,0:T(8,128)}) custom-call(bf16[512,256]{1,0:T(8,128)(2,1)S(1)} %get-tuple-element.6.a, bf16[512,896]{1,0:T(8,128)(2,1)S(1)} %get-tuple-element.7.b, f32[256,896]{1,0:T(8,128)S(1)} %get-tuple-element.8.d), custom_call_target="tpu_custom_call" | custom-call | tf_op jit(solution)/shard_map/pallas_call | solution.py:595

commit v6 on v5

--- a/solution.py
+++ b/solution.py
@@ -457,21 +457,21 @@
     z_pair(4, 0)
     acc[...] = jnp.dot(cot[0], w[pl.ds(0, feat), :], preferred_element_type=F32)
     lax.fori_loop(1, 4, h_part, 0)
+    z_pair(5, 0)
     z_pair(4, 1)
     xo_end(0, 0)
     go(yo, 0)
-    lax.fori_loop(4, 9, h_part, 0)
-    z_pair(5, 0)
-    lax.fori_loop(9, 13, h_part, 0)
+    lax.fori_loop(4, 8, h_part, 0)
     z_pair(5, 1)
+    z_pair(6, 0)
     xo_end(0, 1)
     go(yo, 1)
-    lax.fori_loop(13, 16, h_part, 0)
+    lax.fori_loop(8, 12, h_part, 0)
+    z_pair(6, 1)
+    lax.fori_loop(12, 16, h_part, 0)
     hgb[...] = acc[...].astype(BF16)
     st_hg = pltpu.make_async_copy(hgb, hidden_grad, store_sem.at[0])
     st_hg.start()
-    z_pair(6, 0)
-    z_pair(6, 1)
     xo_end(1, 0)
     xo_end(1, 1)
 

time: 80 us -> 79.1 us (0.989)
  the two profiles are of different devices: /device:TPU:1 before, /device:TPU:9 now
where the time goes in v6:
time: 79.1 us; the launch traced here: 79 us
  Pallas kernels  78.4 us (99%)
    pallas_call x1, Pallas kernels, shards(): pl.pallas_call(functools.partial(kernel, scale), out_shape=tuple((v(*shap...  77.1 us

profile of v6, /device:TPU:9, one launch (start us, length us, event | category | flops | bytes accessed | tf_op | source)
XLA Modules:
  0.0 79.0 jit_solution(14511463877378718196)
XLA Ops:
  0.6 77.1 %shard_map.58 = (bf16[512,256]{1,0:T(8,128)(2,1)S(1)}, bf16[512,896]{1,0:T(8,128)(2,1)S(1)}, f32[256,896]{1,0:T(8,128)S(1)}) custom-call(bf16[512,896]{1,0:T(8,128)(2,1)} %hidden.1, bf16[4096,896]{1,0:T(8,128)(2,1)} %weight.1, bf16[512,256]{1,0:T(8,128)(2,1)} %cotangent.1), custom_call_target="tpu_custom_call" | custom-call | tf_op jit(solution)/shard_map/pallas_call | solution.py:552
  77.7 1.3 %shard_map.59 = (bf16[512,256]{1,0:T(8,128)(2,1)}, bf16[512,896]{1,0:T(8,128)(2,1)}, f32[256,896]{1,0:T(8,128)}) custom-call(bf16[512,256]{1,0:T(8,128)(2,1)S(1)} %get-tuple-element.6.a, bf16[512,896]{1,0:T(8,128)(2,1)S(1)} %get-tuple-element.7.b, f32[256,896]{1,0:T(8,128)S(1)} %get-tuple-element.8.d), custom_call_target="tpu_custom_call" | custom-call | tf_op jit(solution)/shard_map/pallas_call | solution.py:595
